TPU v7x, 8 devices: a whole 2x2x1 slice. The times are simulated.
8 devices in a mesh: fsdp: 8 (over z, y, x, core).
Axes of the slice: x: 2, y: 2, z: 1, core: 2. Of those that a mesh axis runs over, the one named last changes fastest.
Arguments:
- tok_ids: int32 [16384], P('fsdp')
- tok_labels: int32 [16384], P('fsdp')
- loss_mask: int32 [16384], P('fsdp')
- emb_table: bfloat16 [32768, 256], P('fsdp')
- gain_mlp: float32 [256], replicated
- gain_head: float32 [256], replicated
- w_gate: bfloat16 [256, 2048], P('fsdp')
- w_up: bfloat16 [256, 2048], P('fsdp')
- w_down: bfloat16 [2048, 256], P('fsdp')
Outputs:
- output 1: float32 [], replicated
- output 2: float32 [32768, 256], P('fsdp')
- output 3: float32 [256, 2048], P('fsdp')
- output 4: float32 [256, 2048], P('fsdp')
- output 5: float32 [2048, 256], P('fsdp')
All inputs are finite; a program needn't handle non-finite values.
Results may differ from a plain program's by a relative error of at most 0.00867396.
Values are sent between devices in bfloat16 or wider.
A program may use at most 1 GiB of HBM per device.

v0:
```python
import jax
import jax.numpy as jnp
from jax import lax
from jax.sharding import PartitionSpec as P

NORM_EPS = 1e-6
ROW_CONTRACT = (((1,), (1,)), ((), ()))
TOK_CONTRACT = (((0,), (0,)), ((), ()))


def rms_scale(rows_wide, norm_gain):
    inv_rms = lax.rsqrt(jnp.mean(rows_wide * rows_wide, axis=-1, keepdims=True) + NORM_EPS)
    return (rows_wide * inv_rms * norm_gain).astype(jnp.bfloat16), inv_rms


def rms_back(rows_wide, inv_rms, norm_gain, grad_out):
    scaled_grad = grad_out * norm_gain
    return inv_rms * (scaled_grad - rows_wide * (inv_rms * inv_rms) * jnp.mean(scaled_grad * rows_wide, axis=-1, keepdims=True))


def mlp_forward(emb_rows, gain_mlp, gain_head, w_gate, w_up, w_down):
    emb_wide = emb_rows.astype(jnp.float32)
    a_norm, inv_first = rms_scale(emb_wide, gain_mlp)
    gate_wide = jnp.dot(a_norm, w_gate, preferred_element_type=jnp.float32).astype(jnp.bfloat16).astype(jnp.float32)
    up_wide = jnp.dot(a_norm, w_up, preferred_element_type=jnp.float32).astype(jnp.bfloat16).astype(jnp.float32)
    gate_sig = jax.nn.sigmoid(gate_wide)
    act_rows = (gate_wide * gate_sig * up_wide).astype(jnp.bfloat16)
    hid_wide = (emb_wide + jnp.dot(act_rows, w_down, preferred_element_type=jnp.float32)).astype(jnp.bfloat16).astype(jnp.float32)
    h_norm, inv_second = rms_scale(hid_wide, gain_head)
    return (emb_wide, inv_first, a_norm, gate_wide, up_wide, gate_sig, act_rows, hid_wide, inv_second), h_norm


def head_forward(h_norm, emb_table, tok_labels, tok_coef):
    logits = lax.dot_general(h_norm, emb_table, ROW_CONTRACT, preferred_element_type=jnp.float32)
    row_max = jnp.max(logits, axis=-1, keepdims=True)
    exp_rows = jnp.exp(logits - row_max)
    sum_exp = jnp.sum(exp_rows, axis=-1, keepdims=True)
    is_label = jnp.arange(logits.shape[1])[None, :] == tok_labels[:, None]
    picked = jnp.sum(jnp.where(is_label, logits, 0.0), axis=-1)
    tok_loss = row_max[:, 0] + jnp.log(sum_exp[:, 0]) - picked
    d_logits = ((exp_rows / sum_exp - is_label.astype(jnp.float32)) * tok_coef[:, None]).astype(jnp.bfloat16)
    return jnp.sum(tok_coef * tok_loss), d_logits


def mlp_backward(saved, d_hidden, gain_mlp, w_gate, w_up, w_down):
    emb_wide, inv_first, a_norm, gate_wide, up_wide, gate_sig, act_rows = saved[:7]
    hid_grad = d_hidden.astype(jnp.bfloat16)
    d_act = lax.dot_general(hid_grad, w_down, ROW_CONTRACT, preferred_element_type=jnp.float32)
    grad_down = lax.dot_general(act_rows, hid_grad, TOK_CONTRACT, preferred_element_type=jnp.float32)
    d_up = (d_act * gate_wide * gate_sig).astype(jnp.bfloat16)
    d_gate = (d_act * up_wide * gate_sig * (1.0 + gate_wide * (1.0 - gate_sig))).astype(jnp.bfloat16)
    grad_gate = lax.dot_general(a_norm, d_gate, TOK_CONTRACT, preferred_element_type=jnp.float32)
    grad_up = lax.dot_general(a_norm, d_up, TOK_CONTRACT, preferred_element_type=jnp.float32)
    d_anorm = lax.dot_general(d_gate, w_gate, ROW_CONTRACT, preferred_element_type=jnp.float32) + lax.dot_general(d_up, w_up, ROW_CONTRACT, preferred_element_type=jnp.float32)
    grad_x = d_hidden + rms_back(emb_wide, inv_first, gain_mlp, d_anorm)
    return grad_x, grad_gate, grad_up, grad_down


def solution(mesh):
    def gather_rows(row_shard):
        return lax.all_gather(row_shard, "fsdp", axis=0, tiled=True)

    def scatter_rows(full_rows):
        return lax.psum_scatter(full_rows, "fsdp", scatter_dimension=0, tiled=True)

    def device_step(tok_ids, tok_labels, loss_mask, table_shard, gain_mlp, gain_head, gate_shard, up_shard, down_shard):
        mask_wide = loss_mask.astype(jnp.float32)
        tok_coef = mask_wide / lax.psum(jnp.sum(mask_wide), "fsdp")
        table_full = gather_rows(table_shard)
        gate_full = gather_rows(gate_shard)
        up_full = gather_rows(up_shard)
        down_full = gather_rows(down_shard)
        emb_rows = jnp.take(table_full, tok_ids, axis=0)
        saved, h_norm = mlp_forward(emb_rows, gain_mlp, gain_head, gate_full, up_full, down_full)
        loss_part, d_logits = head_forward(h_norm, table_full, tok_labels, tok_coef)
        table_again, d_logits = lax.optimization_barrier((table_shard, d_logits))
        table_back = gather_rows(table_again)
        d_hnorm = jnp.dot(d_logits, table_back, preferred_element_type=jnp.float32)
        head_grad = lax.dot_general(d_logits, h_norm, TOK_CONTRACT, preferred_element_type=jnp.float32)
        d_hidden = rms_back(saved[7], saved[8], gain_head, d_hnorm)
        gate_again, up_again, down_again, d_hidden = lax.optimization_barrier((gate_shard, up_shard, down_shard, d_hidden))
        gate_back = gather_rows(gate_again)
        up_back = gather_rows(up_again)
        down_back = gather_rows(down_again)
        grad_x, grad_gate, grad_up, grad_down = mlp_backward(saved, d_hidden, gain_mlp, gate_back, up_back, down_back)
        grad_table = head_grad + jax.ops.segment_sum(grad_x, tok_ids, num_segments=table_back.shape[0])
        return (lax.psum(loss_part, "fsdp"), scatter_rows(grad_table), scatter_rows(grad_gate), scatter_rows(grad_up), scatter_rows(grad_down))

    row_spec = P("fsdp", None)
    tok_spec = P("fsdp")
    return jax.shard_map(device_step, mesh=mesh, in_specs=(tok_spec, tok_spec, tok_spec, row_spec, P(), P(), row_spec, row_spec, row_spec), out_specs=(P(), row_spec, row_spec, row_spec, row_spec), check_vma=False)
```

profile of v0, /device:TPU:0, one launch (start us, length us, event | category | flops | bytes accessed | tf_op | source)
XLA Modules:
  0.0 990.2 jit_solution(2286650762684241366)
XLA Ops:
  7.2 0.0 copy-start.19
  7.2 0.0 all-gather.9.cloned.1.call-start
  7.2 0.7 all-gather.9.cloned.1.call-update
  7.9 0.0 all-gather.11.cloned.1.call-start
  8.0 0.7 all-gather.11.cloned.1.call-update
  8.7 0.0 all-gather.13.cloned.1.call-start
  8.7 0.7 all-gather.13.cloned.1.call-update
  9.4 0.0 all-gather.15.cloned.1.call-start
  9.4 0.5 all-gather.15.cloned.1.call-update
  10.0 0.0 all-gather.17.cloned.1.call-start
  10.0 1.3 convert_reduce_fusion
  11.3 0.7 fusion.36
  12.0 0.7 compare_and_fusion
  12.7 25.9 %psum.14 = f32[]{:T(128)} all-reduce(f32[]{:T(128)} %convert_reduce_fusion), channel_id=1, replica_groups=mesh['fsdp'=8] {'fsdp'}, use_global_device_ids=true, to_apply=%region_1.0 | all-reduce | flops 1 | bytes 8 | tf_op jit(solution)/shard_map/psum | solution.py:68
  38.6 59.2 %all-gather.9.cloned.1.call-done = bf16[32768,256]{1,0:T(8,128)(2,1)} async-done(((bf16[4096,256]{1,0:T(8,128)(2,1)}), bf16[32768,256]{1,0:T(8,128)(2,1)}) %all-gather.9.cloned.1.call-update) | async-done | bytes 16777232 | tf_op jit(solution)/shard_map/all_gather | solution.py:61
  97.8 14.6 %gather_fusion = bf16[2048,256]{1,0:T(8,128)(2,1)S(1)} fusion(bf16[32768,256]{1,0:T(8,128)(2,1)} %all-gather.9.cloned.1.call-done, s32[2048]{0:T(1024)S(1)} %fusion.36), kind=kCustom, calls=%fused_computation | custom fusion | bytes 2105344 | tf_op jit(solution)/shard_map/jit(_take)/gather | solution.py:73
  112.4 0.6 copy.15
  113.0 0.3 fusion.20
  113.3 0.7 fusion.37
  114.0 3.2 all-gather.11.cloned.1.call-done
  117.2 7.0 convolution_convert_fusion.1
  124.2 12.4 %all-gather.13.cloned.1.call-done = bf16[256,2048]{1,0:T(8,128)(2,1)} async-done(((bf16[32,2048]{1,0:T(8,128)(2,1)}), bf16[256,2048]{1,0:T(8,128)(2,1)}) %all-gather.13.cloned.1.call-update) | async-done | bytes 1048592 | tf_op jit(solution)/shard_map/all_gather | solution.py:61
  136.6 11.3 %fusion.1 = (bf16[2048,2048]{1,0:T(8,128)(2,1)}, bf16[2048,2048]{1,0:T(8,128)(2,1)}) fusion(bf16[2048,2048]{1,0:T(8,128)(2,1)} %convolution_convert_fusion.1, bf16[256,2048]{1,0:T(8,128)(2,1)} %all-gather.13.cloned.1.call-done, f32[256]{0:T(256)S(1)} %copy-done.19, f32[2048]{0:T(1024)S(1)} %get-tuple-element.24, bf16[2048,256]{0,1:T(8,128)(2,1)S(1)} %copy.15, ...), kind=kOutput, calls=%fused_computation.13 | convolution fusion | flops 2187853824 | bytes 27274240 | tf_op jit(solution)/shard_map/dot_general | solution.py:25
  147.9 7.9 all-gather.15.cloned.1.call-done
  155.9 6.1 fusion.13
  162.0 0.7 fusion.38
  162.7 93.1 %fusion.45 = (f32[2048]{0:T(1024)S(1)}, f32[2048,32768]{1,0:T(8,128)}) fusion(bf16[32768,256]{1,0:T(8,128)(2,1)} %all-gather.9.cloned.1.call-done, bf16[2048,256]{0,1:T(8,128)(2,1)S(1)} %get-tuple-element.30, f32[256]{0:T(256)S(1)} %copy-done.8, f32[2048]{0:T(1024)S(1)} %get-tuple-element.26), kind=kOutput, calls=%fused_computation.74 | convolution fusion | flops 34428944384 | bytes 286278656 | tf_op jit(solution)/shard_map/dot_general | solution.py:34
  255.8 94.0 %fusion = (f32[2048]{0:T(1024)S(1)}, f32[2048]{0:T(1024)S(1)}) fusion(f32[2048,32768]{1,0:T(8,128)} %get-tuple-element.32, f32[2048]{0:T(1024)S(1)} %get-tuple-element.31, s32[2048]{0:T(1024)S(1)} %copy-done.15), kind=kLoop, calls=%fused_computation.6 | loop fusion | flops 335540224 | bytes 268468224 | tf_op jit(solution)/shard_map/reduce_sum | solution.py:37
  349.8 1.3 multiply_reduce_fusion
  351.1 127.2 %multiply_convert_fusion = bf16[2048,32768]{1,0:T(8,128)(2,1)} fusion(f32[2048,32768]{1,0:T(8,128)} %get-tuple-element.32, f32[2048]{0:T(1024)S(1)} %get-tuple-element.20, f32[2048]{0:T(1024)S(1)} %get-tuple-element.17, s32[2048]{0:T(1024)S(1)} %copy-done.15, f32[2048]{0:T(1024)S(1)} %get-tuple-element.31), kind=kLoop, calls=%fused_computation.2 | loop fusion | flops 469762048 | bytes 402685952 | tf_op jit(solution)/shard_map/convert_element_type | solution.py:41
  478.3 0.0 all-gather.17.cloned.1.call-update
  478.3 0.0 copy-start.7
  478.3 0.0 copy-start.17
  478.3 0.0 all-gather.19.cloned.1.call-start
  478.4 84.1 %all-gather.17.cloned.1.call-done = bf16[32768,256]{1,0:T(8,128)(2,1)} async-done(((bf16[4096,256]{1,0:T(8,128)(2,1)}), bf16[32768,256]{1,0:T(8,128)(2,1)}) %all-gather.17.cloned.1.call-update) | async-done | bytes 16777232 | tf_op jit(solution)/shard_map/all_gather | solution.py:61
  562.5 52.6 %fusion.19 = (f32[2048]{0:T(1024)S(1)}, f32[2048,256]{0,1:T(8,128)}) fusion(bf16[2048,256]{0,1:T(8,128)(2,1)S(1)} %copy-done.3, f32[256]{0:T(256)S(1)} %copy-done.9, bf16[2048,32768]{1,0:T(8,128)(2,1)} %multiply_convert_fusion, bf16[32768,256]{1,0:T(8,128)(2,1)} %all-gather.17.cloned.1.call-done), kind=kOutput, calls=%fused_computation.44 | convolution fusion | flops 34361835520 | bytes 154149888 | tf_op jit(solution)/shard_map/dot_general | solution.py:78
  615.2 2.0 fusion.18
  617.1 0.0 all-gather.19.cloned.1.call-update
  617.2 0.0 all-gather.21.cloned.1.call-start
  617.2 0.7 all-gather.21.cloned.1.call-update
  617.9 0.0 all-gather.23.cloned.1.call-start
  618.0 0.7 all-gather.23.cloned.1.call-update
  618.7 0.3 reduce-scatter.11.cloned.1.call-start
  618.9 7.3 fusion.28
  626.2 0.0 reduce-scatter.11.cloned.1.call-update
  626.2 0.0 reduce-scatter.9.cloned.1.call-start
  626.3 8.6 all-gather.19.cloned.1.call-done
  634.9 17.8 %fusion.10 = (bf16[2048,2048]{1,0:T(8,128)(2,1)}, bf16[2048,2048]{1,0:T(8,128)(2,1)}) fusion(bf16[2048,2048]{1,0:T(8,128)(2,1)} %convolution_convert_fusion.1, bf16[2048,2048]{1,0:T(8,128)(2,1)} %get-tuple-element.28, bf16[2048,256]{1,0:T(8,128)(2,1)} %all-gather.19.cloned.1.call-done, f32[2048,256]{0,1:T(8,128)} %copy-done.4), kind=kOutput, calls=%fused_computation.22 | convolution fusion | flops 2210922496 | bytes 36700160 | tf_op jit(solution)/shard_map/dot_general | solution.py:48
  652.7 7.1 fusion.39
  659.8 0.0 reduce-scatter.9.cloned.1.call-update
  659.8 0.0 reduce-scatter.7.cloned.1.call-start
  659.9 7.1 fusion.41
  666.9 0.0 reduce-scatter.7.cloned.1.call-update
  667.0 0.3 reduce-scatter.5.cloned.1.call-start
  667.3 60.2 %fusion.32 = f32[32768,256]{1,0:T(8,128)} fusion(bf16[2048,32768]{1,0:T(8,128)(2,1)} %multiply_convert_fusion, bf16[2048,256]{0,1:T(8,128)(2,1)S(1)} %copy-done.3, f32[256]{0:T(256)S(1)} %copy-done.9, f32[2048]{0:T(1024)S(1)} %copy-done.7), kind=kOutput, calls=%fused_computation.58 | convolution fusion | flops 34361835520 | bytes 168829952 | tf_op jit(solution)/shard_map/dot_general | solution.py:79
  727.4 7.3 fusion.46
  734.7 6.9 fusion.27
  741.7 2.0 fusion.26
  743.7 1.9 copy.16
  745.7 33.4 %scatter_fusion = f32[32768,256]{1,0:T(8,128)} fusion(f32[32768,256]{1,0:T(8,128)} %fusion.32, s32[2048]{0:T(1024)S(1)} %copy-done.14, f32[2048,256]{1,0:T(8,128)S(1)} %copy.16), kind=kCustom, calls=%fused_computation.1 | custom fusion | flops 524288 | bytes 6299648 | tf_op jit(solution)/shard_map/scatter-add | solution.py:86
  779.0 0.0 reduce-scatter.5.cloned.1.call-update
  779.0 22.5 %psum.15 = f32[]{:T(128)} all-reduce(f32[]{:T(128)} %get-tuple-element.19), channel_id=1, replica_groups=mesh['fsdp'=8] {'fsdp'}, use_global_device_ids=true, to_apply=%region_8.9 | all-reduce | flops 1 | bytes 8 | tf_op jit(solution)/shard_map/psum | solution.py:87
  801.5 0.0 reduce-scatter.7.cloned.1.call-done
  801.5 181.3 %reduce-scatter.5.cloned.1.call-done = f32[4096,256]{1,0:T(8,128)} async-done(((f32[32768,256]{1,0:T(8,128)}), f32[4096,256]{1,0:T(8,128)}) %reduce-scatter.5.cloned.1.call-update) | async-done | bytes 4194320 | tf_op jit(solution)/shard_map/reduce_scatter | solution.py:64
  (45 shorter events, 0.1 us)
Async XLA Ops:
  7.2 110.0 %copy-start.19 = (f32[256]{0:T(256)S(1)}, f32[256]{0:T(256)}, u32[]{:S(2)}) copy-start(f32[256]{0:T(256)} %param.13) | copy-start | bytes 3076
  7.2 90.6 %all-gather.9.cloned.1.call-start = ((), (), s32[]{:S(2)}) async-start(), calls=%async_computation.4 | async-start | bytes 18874368 | tf_op jit(solution)/shard_map/all_gather | solution.py:61
  7.9 109.3 %all-gather.11.cloned.1.call-start = ((), (), s32[]{:S(2)}) async-start(), calls=%async_computation.5 | async-start | bytes 1179648 | tf_op jit(solution)/shard_map/all_gather | solution.py:61
  8.7 127.9 %all-gather.13.cloned.1.call-start = ((), (), s32[]{:S(2)}) async-start(), calls=%async_computation.6 | async-start | bytes 1179648 | tf_op jit(solution)/shard_map/all_gather | solution.py:61
  9.4 146.5 %all-gather.15.cloned.1.call-start = ((), (), s32[]{:S(2)}) async-start(), calls=%async_computation.7 | async-start | bytes 1179648 | tf_op jit(solution)/shard_map/all_gather | solution.py:61
  10.0 552.6 %all-gather.17.cloned.1.call-start = ((), (), s32[]{:S(2)}) async-start(), calls=%async_computation.8 | async-start | bytes 18874368 | tf_op jit(solution)/shard_map/all_gather | solution.py:61
  12.7 143.1 %copy-start.12 = (pred[2048]{0:T(1024)(128)(4,1)}, pred[2048]{0:T(1024)(128)(4,1)S(1)}, u32[]{:S(2)}) copy-start(pred[2048]{0:T(1024)(128)(4,1)S(1)} %compare_and_fusion) | copy-start | bytes 6148
  113.0 42.8 %copy-start = (bf16[2048,256]{0,1:T(8,128)(2,1)}, bf16[2048,256]{0,1:T(8,128)(2,1)S(1)}, u32[]{:S(2)}) copy-start(bf16[2048,256]{0,1:T(8,128)(2,1)S(1)} %copy.15) | copy-start | bytes 3145732
  114.0 33.9 %copy-start.10 = (f32[2048]{0:T(1024)}, f32[2048]{0:T(1024)S(1)}, u32[]{:S(2)}) copy-start(f32[2048]{0:T(1024)S(1)} %get-tuple-element.24) | copy-start | bytes 24580
  155.9 6.8 copy-start.8
  162.0 93.8 %copy-start.2 = (bf16[2048,256]{0,1:T(8,128)(2,1)}, bf16[2048,256]{0,1:T(8,128)(2,1)S(1)}, u32[]{:S(2)}) copy-start(bf16[2048,256]{0,1:T(8,128)(2,1)S(1)} %get-tuple-element.30) | copy-start | bytes 3145732
  162.7 93.2 %copy-start.6 = (f32[2048]{0:T(1024)}, f32[2048]{0:T(1024)S(1)}, u32[]{:S(2)}) copy-start(f32[2048]{0:T(1024)S(1)} %get-tuple-element.26) | copy-start | bytes 24580
  162.7 93.2 %copy-start.15 = (s32[2048]{0:T(1024)S(1)}, s32[2048]{0:T(1024)}, u32[]{:S(2)}) copy-start(s32[2048]{0:T(1024)} %param.10) | copy-start | bytes 24580
  255.8 94.0 %copy-start.18 = (s32[2048]{0:T(1024)S(1)}, s32[2048]{0:T(1024)}, u32[]{:S(2)}) copy-start(s32[2048]{0:T(1024)} %param.11) | copy-start | bytes 24580
  351.1 211.4 %copy-start.3 = (bf16[2048,256]{0,1:T(8,128)(2,1)S(1)}, bf16[2048,256]{0,1:T(8,128)(2,1)}, u32[]{:S(2)}) copy-start(bf16[2048,256]{0,1:T(8,128)(2,1)} %copy-done.2) | copy-start | bytes 3145732
  351.1 211.4 %copy-start.9 = (f32[256]{0:T(256)S(1)}, f32[256]{0:T(256)}, u32[]{:S(2)}) copy-start(f32[256]{0:T(256)} %param.14) | copy-start | bytes 3076
  478.3 136.8 %copy-start.7 = (f32[2048]{0:T(1024)S(1)}, f32[2048]{0:T(1024)}, u32[]{:S(2)}) copy-start(f32[2048]{0:T(1024)} %copy-done.6) | copy-start | bytes 24580
  478.3 136.8 %copy-start.17 = (f32[2048]{0:T(1024)S(1)}, f32[2048]{0:T(1024)}, u32[]{:S(2)}) copy-start(f32[2048]{0:T(1024)} %get-tuple-element.25) | copy-start | bytes 24580
  478.3 156.5 %all-gather.19.cloned.1.call-start = ((), (), s32[]{:S(2)}) async-start(), calls=%async_computation.9 | async-start | bytes 1179648 | tf_op jit(solution)/shard_map/all_gather | solution.py:61
  617.1 9.1 copy-start.4
  617.2 110.3 %all-gather.21.cloned.1.call-start = ((), (), s32[]{:S(2)}) async-start(), calls=%async_computation.10 | async-start | bytes 1179648 | tf_op jit(solution)/shard_map/all_gather | solution.py:61
  617.9 116.8 %all-gather.23.cloned.1.call-start = ((), (), s32[]{:S(2)}) async-start(), calls=%async_computation.11 | async-start | bytes 1179648 | tf_op jit(solution)/shard_map/all_gather | solution.py:61
  618.7 182.9 %reduce-scatter.11.cloned.1.call-start = ((), (), s32[]{:S(2)}) async-start(), calls=%async_computation.15 | async-start | bytes 2359296 | tf_op jit(solution)/shard_map/reduce_scatter | solution.py:64
  626.2 175.3 %reduce-scatter.9.cloned.1.call-start = ((), (), s32[]{:S(2)}) async-start(), calls=%async_computation.14 | async-start | bytes 2359296 | tf_op jit(solution)/shard_map/reduce_scatter | solution.py:64
  634.9 17.8 %copy-start.1 = (bf16[2048,256]{0,1:T(8,128)(2,1)S(1)}, bf16[2048,256]{0,1:T(8,128)(2,1)}, u32[]{:S(2)}) copy-start(bf16[2048,256]{0,1:T(8,128)(2,1)} %copy-done) | copy-start | bytes 3145732
  634.9 17.8 %copy-start.11 = (f32[2048]{0:T(1024)S(1)}, f32[2048]{0:T(1024)}, u32[]{:S(2)}) copy-start(f32[2048]{0:T(1024)} %copy-done.10) | copy-start | bytes 24580
  634.9 17.8 %copy-start.13 = (pred[2048]{0:T(1024)(128)(4,1)S(1)}, pred[2048]{0:T(1024)(128)(4,1)}, u32[]{:S(2)}) copy-start(pred[2048]{0:T(1024)(128)(4,1)} %copy-done.12) | copy-start | bytes 6148
  634.9 17.8 %copy-start.20 = (f32[256]{0:T(256)S(1)}, f32[256]{0:T(256)}, u32[]{:S(2)}) copy-start(f32[256]{0:T(256)} %param.13) | copy-start | bytes 3076
  659.8 141.7 %reduce-scatter.7.cloned.1.call-start = ((), (), s32[]{:S(2)}) async-start(), calls=%async_computation.13 | async-start | bytes 2359296 | tf_op jit(solution)/shard_map/reduce_scatter | solution.py:64
  667.0 315.9 %reduce-scatter.5.cloned.1.call-start = ((), (), s32[]{:S(2)}) async-start(), calls=%async_computation.12 | async-start | bytes 37748736 | tf_op jit(solution)/shard_map/reduce_scatter | solution.py:64
  734.7 7.0 copy-start.16
  734.7 7.0 copy-start.5
  741.7 4.0 copy-start.14
Sparse Core Ops, SparseCore 0:
  9.8 87.9 all-gather.8
  99.6 17.5 all-gather.10
  119.0 17.5 all-gather.12
  138.3 17.5 all-gather.14
  478.4 84.0 all-gather.16
  617.3 17.5 all-gather.18
  636.7 17.5 all-gather.20
  656.1 17.5 all-gather.22
  677.5 32.5 reduce-scatter.10
  713.7 32.5 reduce-scatter.8
  750.1 32.5 reduce-scatter.6
  786.6 196.2 reduce-scatter.4
where the time goes:
time: 999 us; the launch traced here: 990 us
  waiting for transfers between devices  361 us (36%)
  matrix products  284 us (28%)
  other arithmetic  264 us (26%)
  blocking collectives  48.4 us (5%)
  local copies, waits for them, and re-layouts  17.2 us (2%)
  between operations  14.9 us (1%)
    reduce_scatter x4, waiting for transfers between devices, scatter_rows(): return lax.psum_scatter(full_rows, 'fsdp', scatter_dimension=0, tiled=True)  181 us
    all_gather x8, waiting for transfers between devices, gather_rows(): return lax.all_gather(row_shard, 'fsdp', axis=0, tiled=True)  175 us
    convert_element_type x1, other arithmetic, head_forward(): ((exp_rows / sum_exp - is_label.astype(jnp.float32)) * tok_coef[:, None])...  127 us
    reduce_sum x1, other arithmetic, head_forward(): sum_exp = jnp.sum(exp_rows, axis=-1, keepdims=True)  94 us
    dot_general x1, matrix products, head_forward(): lax.dot_general(h_norm, emb_table, ROW_CONTRACT, preferred_element_type=j...  93.1 us
    dot_general x1, matrix products, device_step(): lax.dot_general(d_logits, h_norm, TOK_CONTRACT, preferred_element_type=jn...  60.2 us
    dot_general x1, matrix products, device_step(): d_hnorm = jnp.dot(d_logits, table_back, preferred_element_type=jnp.float32)  52.6 us
    scatter-add x1, other arithmetic, device_step(): jax.ops.segment_sum(grad_x, tok_ids, num_segments=table_back.shape[0])  33.4 us
  transfers between devices with their start and end apart: 12, of which 7 were waited for; matrix products, arithmetic and copies ran while one was open for 19% of the time, Pallas kernels for 0%

commit v1 on v0

v1 whole, which is shorter than its diff:
```python
import functools
import math

import jax
import jax.numpy as jnp
from jax import lax
from jax.experimental import pallas as pl
from jax.experimental.pallas import tpu as pltpu
from jax.sharding import PartitionSpec as P

NORM_EPS = 1e-6
ROW_CONTRACT = (((1,), (1,)), ((), ()))
TOK_CONTRACT = (((0,), (0,)), ((), ()))
MESH = pl.DeviceIdType.MESH
LOG2E = math.log2(math.e)
LN2 = math.log(2.0)
N_DEV = 8
UNIT = 256
V_CHUNK = 512
VMEM_MAX = 67_043_328


def peer_of(me, step):
    core = (me % 2 + step % 2) % 2
    col = ((me // 2) % 2 + (step // 2) % 2) % 2
    row = (me // 4 + step // 4) % 2
    return row * 4 + col * 2 + core


def pair_xor(pair, other):
    return ((pair // 2 + other // 2) % 2) * 2 + (pair % 2 + other % 2) % 2


def meet_all(me):
    barrier = pltpu.get_barrier_semaphore()
    for step in range(1, N_DEV):
        pl.semaphore_signal(barrier, inc=1, device_id=(peer_of(me, step),), device_id_type=MESH)
    pl.semaphore_wait(barrier, N_DEV - 1)


def remote(src, dst, send_sem, recv_sem, target):
    return pltpu.make_async_remote_copy(src_ref=src, dst_ref=dst, send_sem=send_sem, recv_sem=recv_sem, device_id=(target,), device_id_type=MESH)


def tokens_kernel(tok_hbm, all_ref, local_sem, send_sems, recv_sems):
    me = lax.axis_index("fsdp")
    own = pltpu.make_async_copy(tok_hbm, all_ref.at[0], local_sem)
    own.start()
    meet_all(me)
    own.wait()
    copies = []
    for step in range(1, N_DEV):
        copy = remote(all_ref.at[0], all_ref.at[step], send_sems.at[step], recv_sems.at[step], peer_of(me, step))
        copy.start()
        copies.append(copy)
    for copy in copies:
        copy.wait()


def gather_tokens(tok_block):
    return pl.pallas_call(
        tokens_kernel,
        out_shape=jax.ShapeDtypeStruct((N_DEV,) + tok_block.shape, tok_block.dtype),
        in_specs=[pl.BlockSpec(memory_space=pl.ANY)],
        out_specs=pl.BlockSpec(memory_space=pltpu.VMEM),
        scratch_shapes=[pltpu.SemaphoreType.DMA, pltpu.SemaphoreType.DMA((N_DEV,)), pltpu.SemaphoreType.DMA((N_DEV,))],
        compiler_params=pltpu.CompilerParams(collective_id=0, has_side_effects=True),
        name="gather_tokens",
    )(tok_block)


def head_kernel(groups, vocab, hn_hbm, lab_hbm, norm_ref, table_ref, table_t_ref, dhn_ref, dtable_ref, lse_ref, pick_ref,
                hn_all, lab_all, lse_mine, lse_all, part_own, part_out, part_in, sum_in, dhn_acc,
                local_sems, ag_send, ag_recv, fw_send, lab_send, lab_recv, st_send, st_recv, d2_send, d2_recv, rs_send, rs_recv):
    me = lax.axis_index("fsdp")
    chunks = vocab // V_CHUNK
    pair_rows = 2 * UNIT

    lab_copy = pltpu.make_async_copy(lab_hbm, lab_all.at[0], local_sems.at[0])
    lab_copy.start()
    hn_copy = pltpu.make_async_copy(hn_hbm, hn_all.at[:, 0], local_sems.at[1])
    hn_copy.start()
    meet_all(me)
    lab_copy.wait()

    def label_send(step):
        return remote(lab_all.at[0], lab_all.at[step], lab_send.at[step], lab_recv.at[step], peer_of(me, step))

    def own_send(step, group):
        return remote(hn_all.at[group, 0], hn_all.at[group, step], ag_send.at[step, group], ag_recv.at[step, group], peer_of(me, step))

    def forward(step, group):
        return remote(hn_all.at[group, step], hn_all.at[group, step + 1], fw_send.at[step, group], ag_recv.at[step + 1, group], peer_of(me, 1))

    def stat_send(step, group):
        return remote(lse_mine.at[group], lse_all.at[group, step], st_send.at[step, group], st_recv.at[step, group], peer_of(me, step))

    def part_send(group, pair):
        return remote(part_out.at[group, pair], part_in.at[group, pair], d2_send.at[group, pair], d2_recv.at[group, pair], peer_of(me, 1))

    def home_send(group, pair):
        return remote(part_own.at[group, pair], sum_in.at[group, pair], rs_send.at[group, pair], rs_recv.at[group, pair], peer_of(me, 2 * pair))

    hn_copy.wait()

    @pl.loop(0, groups)
    def _(group):
        for step in (1, 2, 4, 6):
            own_send(step, group).start()

    for step in range(1, N_DEV):
        label_send(step).start()
    dtable_ref[...] = jnp.zeros_like(dtable_ref)
    pick_ref[...] = jnp.zeros_like(pick_ref)

    def table_rows(chunk):
        return table_ref[pl.ds(pl.multiple_of(chunk * V_CHUNK, V_CHUNK), V_CHUNK), :]

    @pl.loop(0, groups)
    def _(group):
        @pl.loop(0, 4)
        def _(pair):
            @pl.when(pair > 0)
            def _():
                own_send(2 * pair, group).wait_recv()
                forward(2 * pair, group).start()

            @pl.when(pair == 0)
            def _():
                own_send(1, group).wait_recv()

            @pl.when(pair > 0)
            def _():
                forward(2 * pair, group).wait_recv()

            tile = hn_all[group, pl.ds(2 * pair, 2)].reshape(pair_rows, 256)
            run_max = jnp.full((8, pair_rows), -jnp.inf, jnp.float32)
            run_sum = jnp.zeros((8, pair_rows), jnp.float32)
            for chunk in range(chunks):
                logits = lax.dot_general(table_rows(chunk), tile, ROW_CONTRACT, preferred_element_type=jnp.float32)
                logits = logits.reshape(V_CHUNK // 8, 8, pair_rows)
                new_max = jnp.maximum(run_max, jnp.max(logits, axis=0))
                new_scaled = new_max * LOG2E
                run_sum = run_sum * jnp.exp2(run_max * LOG2E - new_scaled) + jnp.sum(jnp.exp2(logits * LOG2E - new_scaled[None]), axis=0)
                run_max = new_max
            scaled = run_max * LOG2E
            top = jnp.max(scaled, axis=0, keepdims=True)
            total = jnp.sum(run_sum * jnp.exp2(scaled - top), axis=0, keepdims=True)
            lse_mine[group, pair] = top + jnp.log2(total)

        @pl.when(group > 0)
        def _():
            for step in range(1, N_DEV):
                stat_send(step, group - 1).start()

    for step in range(1, N_DEV):
        label_send(step).wait_recv()

    log2_n = norm_ref[0:1, :]
    log2_n = jnp.concatenate([log2_n] * (pair_rows // 128), axis=1)
    inv_n = norm_ref[1:2, :]
    inv_n = jnp.concatenate([inv_n] * (pair_rows // 128), axis=1)
    row_iota = lax.broadcasted_iota(jnp.int32, (V_CHUNK, pair_rows), 0)

    def finish_pair(group, pair):
        part_send(group, pair).wait_recv()
        part_own[group, pair] = part_own[group, pair] + part_in[group, pair]

    @pl.loop(0, groups)
    def _(group):
        @pl.when(group == 0)
        def _():
            for step in range(1, N_DEV):
                stat_send(step, groups - 1).start()

        for step in range(1, N_DEV):
            stat_send(step, group).wait_recv()

        @pl.loop(0, 4)
        def _(turn):
            pair = 3 - turn
            low, high = [], []
            for step in range(N_DEV):
                source = lse_mine.at[group] if step == 0 else lse_all.at[group, step]
                row = source[pair_xor(pair, step // 2)]
                halves = [row[:, :UNIT], row[:, UNIT:]]
                low.append(halves[step % 2])
                high.append(halves[1 - step % 2])
            both = [jnp.concatenate(two, axis=1) for two in zip(low, high)]
            top = functools.reduce(jnp.maximum, both)
            lse = top + jnp.log2(sum(jnp.exp2(part - top) for part in both))
            label = jnp.concatenate([lab_all[2 * pair, group], lab_all[2 * pair + 1, group]], axis=1)
            valid = label >= 0
            shift = jnp.where(valid, lse + log2_n, 1e30)

            @pl.when(pair == 0)
            def _():
                lse_ref[group] = jnp.where(valid, lse, 0.0)[:, :UNIT]

            tile = hn_all[group, pl.ds(2 * pair, 2)].reshape(pair_rows, 256)
            local_label = label - me * vocab
            picked = jnp.zeros((8, pair_rows), jnp.float32)
            for chunk in range(chunks):
                logits = lax.dot_general(table_rows(chunk), tile, ROW_CONTRACT, preferred_element_type=jnp.float32)
                is_label = row_iota == (local_label - chunk * V_CHUNK)
                picked += jnp.sum(jnp.where(is_label, logits, 0.0).reshape(V_CHUNK // 8, 8, pair_rows), axis=0)
                prob = jnp.exp2(logits * LOG2E - shift)
                d_logits = jnp.where(is_label, prob - inv_n, prob).astype(jnp.bfloat16)
                rows = pl.ds(chunk * V_CHUNK, V_CHUNK)
                dtable_ref[rows, :] += jnp.dot(d_logits, tile, preferred_element_type=jnp.float32)
                d_part = jnp.dot(table_t_ref[:, rows], d_logits, preferred_element_type=jnp.float32)
                if chunk == 0:
                    dhn_acc[...] = d_part
                else:
                    dhn_acc[...] += d_part
            pick_ref[...] += picked
            part_own[group, pair] = dhn_acc[:, :UNIT]
            part_out[group, pair] = dhn_acc[:, UNIT:]
            part_send(group, pair).start()

            @pl.when(turn > 0)
            def _():
                finish_pair(group, pair + 1)
                home_send(group, pair + 1).start()

            @pl.when((turn == 0) & (group > 0))
            def _():
                finish_pair(group - 1, 0)

    finish_pair(groups - 1, 0)

    @pl.loop(0, groups)
    def _(group):
        total = part_own[group, 0]
        for pair in (1, 2, 3):
            home_send(group, pair).wait_recv()
            total = total + sum_in[group, pair]
        dhn_ref[group] = total.T
        for step in (1, 2, 4, 6):
            own_send(step, group).wait_send()
        for step in (2, 4, 6):
            forward(step, group).wait_send()
        for step in range(1, N_DEV):
            stat_send(step, group).wait_send()
        for pair in range(4):
            part_send(group, pair).wait_send()
        for pair in (1, 2, 3):
            home_send(group, pair).wait_send()

    for step in range(1, N_DEV):
        label_send(step).wait_send()


def head_call(h_norm, labels, norm_rows, table, table_t, groups):
    vocab = table.shape[0]
    dma = pltpu.SemaphoreType.DMA
    vmem = pl.BlockSpec(memory_space=pltpu.VMEM)
    hbm = pl.BlockSpec(memory_space=pl.ANY)
    f32, bf16 = jnp.float32, jnp.bfloat16
    tokens = N_DEV * groups * UNIT
    return pl.pallas_call(
        functools.partial(head_kernel, groups, vocab),
        out_shape=(
            jax.ShapeDtypeStruct((groups, UNIT, 256), f32),
            jax.ShapeDtypeStruct((vocab, 256), f32),
            jax.ShapeDtypeStruct((groups, 1, UNIT), f32),
            jax.ShapeDtypeStruct((8, 2 * UNIT), f32),
        ),
        in_specs=[hbm, hbm, vmem, vmem, vmem],
        out_specs=(vmem, vmem, vmem, vmem),
        scratch_shapes=[
            pltpu.VMEM((groups, N_DEV, UNIT, 256), bf16),
            pltpu.VMEM((N_DEV, groups, 1, UNIT), jnp.int32),
            pltpu.VMEM((groups, 4, 1, 2 * UNIT), f32),
            pltpu.VMEM((groups, N_DEV, 4, 1, 2 * UNIT), f32),
            pltpu.VMEM((groups, 4, 256, UNIT), f32),
            pltpu.VMEM((groups, 4, 256, UNIT), f32),
            pltpu.VMEM((groups, 4, 256, UNIT), f32),
            pltpu.VMEM((groups, 4, 256, UNIT), f32),
            pltpu.VMEM((256, 2 * UNIT), f32),
            dma((2,)),
            dma((N_DEV, groups)),
            dma((N_DEV, groups)),
            dma((N_DEV, groups)),
            dma((N_DEV,)),
            dma((N_DEV,)),
            dma((N_DEV, groups)),
            dma((N_DEV, groups)),
            dma((groups, 4)),
            dma((groups, 4)),
            dma((groups, 4)),
            dma((groups, 4)),
        ],
        compiler_params=pltpu.CompilerParams(collective_id=1, has_side_effects=True, vmem_limit_bytes=VMEM_MAX),
        cost_estimate=pl.CostEstimate(flops=8 * tokens * vocab * 256, bytes_accessed=16 * vocab * 256, transcendentals=2 * tokens * vocab),
        name="head",
    )(h_norm, labels, norm_rows, table, table_t)


def rms_scale(rows_wide, norm_gain):
    inv_rms = lax.rsqrt(jnp.mean(rows_wide * rows_wide, axis=-1, keepdims=True) + NORM_EPS)
    return (rows_wide * inv_rms * norm_gain).astype(jnp.bfloat16), inv_rms


def rms_back(rows_wide, inv_rms, norm_gain, grad_out):
    scaled_grad = grad_out * norm_gain
    return inv_rms * (scaled_grad - rows_wide * (inv_rms * inv_rms) * jnp.mean(scaled_grad * rows_wide, axis=-1, keepdims=True))


def mlp_forward(emb_rows, gain_mlp, gain_head, w_gate, w_up, w_down):
    emb_wide = emb_rows.astype(jnp.float32)
    a_norm, inv_first = rms_scale(emb_wide, gain_mlp)
    gate_wide = jnp.dot(a_norm, w_gate, preferred_element_type=jnp.float32).astype(jnp.bfloat16).astype(jnp.float32)
    up_wide = jnp.dot(a_norm, w_up, preferred_element_type=jnp.float32).astype(jnp.bfloat16).astype(jnp.float32)
    gate_sig = jax.nn.sigmoid(gate_wide)
    act_rows = (gate_wide * gate_sig * up_wide).astype(jnp.bfloat16)
    hid_wide = (emb_wide + jnp.dot(act_rows, w_down, preferred_element_type=jnp.float32)).astype(jnp.bfloat16).astype(jnp.float32)
    h_norm, inv_second = rms_scale(hid_wide, gain_head)
    return (emb_wide, inv_first, a_norm, gate_wide, up_wide, gate_sig, act_rows, hid_wide, inv_second), h_norm


def mlp_backward(saved, d_hidden, gain_mlp, w_gate, w_up, w_down):
    emb_wide, inv_first, a_norm, gate_wide, up_wide, gate_sig, act_rows = saved[:7]
    hid_grad = d_hidden.astype(jnp.bfloat16)
    d_act = lax.dot_general(hid_grad, w_down, ROW_CONTRACT, preferred_element_type=jnp.float32)
    grad_down = lax.dot_general(act_rows, hid_grad, TOK_CONTRACT, preferred_element_type=jnp.float32)
    d_up = (d_act * gate_wide * gate_sig).astype(jnp.bfloat16)
    d_gate = (d_act * up_wide * gate_sig * (1.0 + gate_wide * (1.0 - gate_sig))).astype(jnp.bfloat16)
    grad_gate = lax.dot_general(a_norm, d_gate, TOK_CONTRACT, preferred_element_type=jnp.float32)
    grad_up = lax.dot_general(a_norm, d_up, TOK_CONTRACT, preferred_element_type=jnp.float32)
    d_anorm = lax.dot_general(d_gate, w_gate, ROW_CONTRACT, preferred_element_type=jnp.float32) + lax.dot_general(d_up, w_up, ROW_CONTRACT, preferred_element_type=jnp.float32)
    grad_x = d_hidden + rms_back(emb_wide, inv_first, gain_mlp, d_anorm)
    return grad_x, grad_gate, grad_up, grad_down


GROUPS = 7


def solution(mesh):
    def gather_rows(row_shard):
        return lax.all_gather(row_shard, "fsdp", axis=0, tiled=True)

    def scatter_rows(full_rows):
        return lax.psum_scatter(full_rows, "fsdp", scatter_dimension=0, tiled=True)

    def device_step(tok_ids, tok_labels, loss_mask, table_shard, gain_mlp, gain_head, gate_shard, up_shard, down_shard):
        me = lax.axis_index("fsdp")
        vocab, width = table_shard.shape
        vocab_all = vocab * N_DEV
        slots = GROUPS * UNIT
        gate_full, up_full, down_full = gather_rows(gate_shard), gather_rows(up_shard), gather_rows(down_shard)
        block = jnp.stack([tok_ids.reshape(-1, 128), tok_labels.reshape(-1, 128), loss_mask.reshape(-1, 128)])
        every = gather_tokens(block)
        ids, labels, mask = every[:, 0].reshape(-1), every[:, 1].reshape(-1), every[:, 2].reshape(-1)
        count = jnp.sum(mask).astype(jnp.float32)
        owner = ids // vocab
        loads = [jnp.sum(jnp.where(owner == dev, mask, 0)) for dev in range(N_DEV)]
        rounds = (functools.reduce(jnp.maximum, loads) + slots - 1) // slots
        last = jnp.int32(2**31 - 1)
        packed = jnp.where((owner == me) & (mask != 0), (ids - me * vocab) * vocab_all + labels, last)
        packed = jnp.sort(packed)
        most = -(-ids.shape[0] // slots) * slots
        packed = jnp.concatenate([packed, jnp.full((most - ids.shape[0],), last)])
        norm_rows = jnp.zeros((8, 128), jnp.float32).at[0].set(jnp.log2(count)).at[1].set(1.0 / count)
        table_t = table_shard.T

        def one_round(state):
            turn, loss, g_table, g_gate, g_up, g_down = state
            mine = lax.dynamic_slice(packed, (turn * slots,), (slots,))
            valid = mine != last
            row_id = jnp.where(valid, mine // vocab_all, 0)
            label = jnp.where(valid, mine % vocab_all, -1)
            saved, h_norm = mlp_forward(jnp.take(table_shard, row_id, axis=0), gain_mlp, gain_head, gate_full, up_full, down_full)
            d_hnorm, head_grad, lse, picked = head_call(h_norm.reshape(GROUPS, UNIT, width), label.reshape(GROUPS, 1, UNIT), norm_rows, table_shard, table_t, GROUPS)
            d_hidden = rms_back(saved[7], saved[8], gain_head, d_hnorm.reshape(slots, width))
            grad_x, grad_gate, grad_up, grad_down = mlp_backward(saved, d_hidden, gain_mlp, gate_full, up_full, down_full)
            in_grad = jax.ops.segment_sum(grad_x, row_id, num_segments=vocab)
            part = (jnp.sum(lse) * LN2 - jnp.sum(picked)) / count
            return (turn + 1, loss + part, g_table + head_grad + in_grad, g_gate + grad_gate, g_up + grad_up, g_down + grad_down)

        zeros = (jnp.int32(0), jnp.float32(0), jnp.zeros((vocab, width), jnp.float32), jnp.zeros(gate_full.shape, jnp.float32), jnp.zeros(up_full.shape, jnp.float32), jnp.zeros(down_full.shape, jnp.float32))
        _, loss, g_table, g_gate, g_up, g_down = lax.while_loop(lambda state: state[0] < rounds, one_round, zeros)
        return (lax.psum(loss, "fsdp"), g_table, scatter_rows(g_gate), scatter_rows(g_up), scatter_rows(g_down))

    row_spec = P("fsdp", None)
    tok_spec = P("fsdp")
    return jax.shard_map(device_step, mesh=mesh, in_specs=(tok_spec, tok_spec, tok_spec, row_spec, P(), P(), row_spec, row_spec, row_spec), out_specs=(P(), row_spec, row_spec, row_spec, row_spec), check_vma=False)
```

time: 999 us -> 566 us (0.57)
  Pallas kernels: 0 us -> 254 us
  waiting for transfers between devices: 361 us -> 112 us
  matrix products: 284 us -> 54.7 us
  other arithmetic: 264 us -> 48.1 us
  blocking collectives: 48.4 us -> 23.7 us
  loops' own time: 0 us -> 24.1 us
    pallas_call x0 -> x2, Pallas kernels: none -> 254 us  [the longest x1 245 us: head_call(): pl.pallas_call(functools.partial(head_kernel, groups, vocab), out_shape=(...]
    dot_general x3 -> x0, matrix products: 206 us -> none  [the longest x1 93.1 us: head_forward(): lax.dot_general(h_norm, emb_table, ROW_CONTRACT, preferred_element_type=j...]
    all_gather x8 -> x3, waiting for transfers between devices: 175 us -> 26.9 us  [gather_rows(): return lax.all_gather(row_shard, 'fsdp', axis=0, tiled=True)]
    convert_element_type x1, other arithmetic: 127 us -> 2.47 us  [rms_scale(): return ((rows_wide * inv_rms * norm_gain).astype(jnp.bfloat16), inv_rms)]
    reduce_scatter x4 -> x3, waiting for transfers between devices: 181 us -> 81.6 us  [scatter_rows(): return lax.psum_scatter(full_rows, 'fsdp', scatter_dimension=0, tiled=True)]
    reduce_sum x3 -> x4, other arithmetic: 96.6 us -> 6.7 us  [the longest x2 2.84 us: one_round(): part = (jnp.sum(lse) * LN2 - jnp.sum(picked)) / count]
    psum x2 -> x1, blocking collectives: 48.4 us -> 23.7 us  [device_step(): lax.psum(loss, 'fsdp')]
    another operation x0 -> x1, loops' own time: none -> 24.1 us  [device_step(): lax.while_loop(lambda state: state[0] < rounds, one_round, zeros)]
  transfers between devices with their start and end apart: 12 -> 6, of which waited for: 7 -> 5; matrix products, arithmetic and copies ran while one was open for 19% -> 3% of each run, Pallas kernels for 0% -> 2%
where the time goes in v1:
time: 566 us; the launch traced here: 559 us
  Pallas kernels  254 us (45%)
  waiting for transfers between devices  112 us (20%)
  matrix products  54.7 us (10%)
  other arithmetic  48.1 us (8%)
  loops' own time  24.1 us (4%)
  blocking collectives  23.7 us (4%)
  local copies, waits for them, and re-layouts  21.9 us (4%)
  between operations  20.4 us (4%)
    pallas_call x1, Pallas kernels, head_call(): pl.pallas_call(functools.partial(head_kernel, groups, vocab), out_shape=(...  245 us
    reduce_scatter x3, waiting for transfers between devices, scatter_rows(): return lax.psum_scatter(full_rows, 'fsdp', scatter_dimension=0, tiled=True)  81.6 us
    all_gather x3, waiting for transfers between devices, gather_rows(): return lax.all_gather(row_shard, 'fsdp', axis=0, tiled=True)  26.9 us
    another operation x1, loops' own time, device_step(): lax.while_loop(lambda state: state[0] < rounds, one_round, zeros)  24.1 us
    psum x1, blocking collectives, device_step(): lax.psum(loss, 'fsdp')  23.7 us
    scatter-add x1, other arithmetic, one_round(): in_grad = jax.ops.segment_sum(grad_x, row_id, num_segments=vocab)  18.4 us
    dot_general x1, matrix products, mlp_backward(): lax.dot_general(hid_grad, w_down, ROW_CONTRACT, preferred_element_type=jn...  12.6 us
  transfers between devices with their start and end apart: 6, of which 5 were waited for; matrix products, arithmetic and copies ran while one was open for 3% of the time, Pallas kernels for 2%

profile of v1, /device:TPU:0, one launch (start us, length us, event | category | flops | bytes accessed | tf_op | source)
XLA Modules:
  0.0 558.5 jit_solution(1831095072830439211)
XLA Ops:
  7.2 0.0 all-gather.4.cloned.1.call-start
  7.2 0.7 all-gather.4.cloned.1.call-update
  7.9 0.0 all-gather.6.cloned.1.call-start
  7.9 0.7 all-gather.6.cloned.1.call-update
  8.6 0.0 all-gather.8.cloned.1.call-start
  8.7 0.7 all-gather.8.cloned.1.call-update
  9.4 0.0 reduce-scatter.8.cloned.1.call-start
  9.4 1.3 pad_add_fusion.tok_hbm
  10.8 8.5 %gather_tokens.1 = s32[8,3,16,128]{3,2,1,0:T(8,128)} custom-call(s32[3,16,128]{2,1,0:T(8,128)} %pad_add_fusion.tok_hbm), custom_call_target="tpu_custom_call" | custom-call | tf_op jit(solution)/shard_map/gather_tokens/pallas_call | solution.py:61
  19.2 1.8 slice_reduce_fusion
  26.9 4.1 copy.16
  31.0 0.9 broadcast_compare_fusion
  31.9 0.1 add_select_fusion.4
  31.9 7.7 %sort.15 = (s32[16384]{0:T(1024)S(1)}, s32[16384]{0:T(1024)}) sort(s32[16384]{0:T(1024)S(1)} %add_select_fusion.4, s32[16384]{0:T(1024)S(1)} %iota.3), dimensions={0}, to_apply=%region_8.9 | sort | flops 229376 | bytes 262144 | tf_op jit(solution)/shard_map/jit(sort)/sort | solution.py:361
  39.7 0.7 scatter.13
  40.4 1.3 scatter.14
  41.6 0.6 concatenate.7
  42.3 7.5 %all-gather.6.cloned.1.call-done = bf16[256,2048]{1,0:T(8,128)(2,1)} async-done(((bf16[32,2048]{1,0:T(8,128)(2,1)}), bf16[256,2048]{1,0:T(8,128)(2,1)}) %all-gather.6.cloned.1.call-update) | async-done | bytes 1048592 | tf_op jit(solution)/shard_map/all_gather | solution.py:341
  49.7 19.4 %all-gather.8.cloned.1.call-done = bf16[2048,256]{1,0:T(8,128)(2,1)} async-done(((bf16[256,256]{1,0:T(8,128)(2,1)}), bf16[2048,256]{1,0:T(8,128)(2,1)}) %all-gather.8.cloned.1.call-update) | async-done | bytes 1048592 | tf_op jit(solution)/shard_map/all_gather | solution.py:341
  69.1 1.5 broadcast.270.clone
  70.7 1.4 broadcast_in_dim.61
  72.1 1.7 broadcast.270
  73.8 2.3 broadcast.269
  76.1 0.2 copy-done.2
  76.2 368.5 %while.22 = (s32[]{:T(128)}, f32[]{:T(128)}, f32[4096,256]{1,0:T(8,128)}, f32[256,2048]{1,0:T(8,128)}, f32[256,2048]{1,0:T(8,128)}, /*index=5*/f32[2048,256]{1,0...) while((s32[]{:T(128)}, f32[]{:T(128)}, ...), condition=%wide.region_18.19_spmd, body=%wide.region_10.0_spmd.sunk | while | flops 137292939264 | bytes 360847200 | solution.py:382
  98.6 0.8 fusion.111
  99.4 0.8 compare_and_fusion.2
  100.3 0.6 reshape.143.lab_hbm
  100.9 0.0 copy-done.19
  100.9 5.5 gather_fusion
  106.4 0.0 copy-start
  106.4 0.6 fusion.112
  107.0 0.6 fusion.113
  107.6 4.3 convolution_convert_fusion.3
  111.9 8.3 %fusion.114 = (bf16[1792,2048]{1,0:T(8,128)(2,1)S(1)}, bf16[1792,2048]{1,0:T(8,128)(2,1)}) fusion(bf16[1792,2048]{1,0:T(8,128)(2,1)S(1)} %convolution_convert_fusion.3, bf16[256,2048]{1,0:T(8,128)(2,1)S(1)} %copy-done.21, f32[256]{0:T(256)} %get-tuple-element.520, f32[1792]{0:T(1024)S(1)} %get-tuple-element.448, ...), kind=kOutput, calls=%fused_computation.8.clone.1 | convolution fusion | flops 1914372096 | bytes 23996160 | tf_op jit(solution)/shard_map/while/body/dot_general | solution.py:314
  120.3 3.3 fusion.115
  123.6 0.6 fusion.116
  124.2 0.6 copy-done.16
  124.8 2.5 fusion.117
  127.3 245.3 %head.4 = (f32[7,256,256]{2,1,0:T(8,128)}, f32[4096,256]{1,0:T(8,128)}, f32[7,1,256]{2,1,0:T(1,128)}, f32[8,512]{1,0:T(8,128)}) custom-call(bf16[7,256,256]{2,1,0:T(8,128)(2,1)} %bitcast.57, s32[7,1,256]{2,1,0:T(1,128)} %reshape.143.lab_hbm, f32[8,128]{1,0:T(8,128)} %get-tuple-element.525.norm_ref, bf16[4096,256]{1,0:T(8,128)(2,1)} %get-tuple-element.563, ...), custom_call_target="tpu_custom_call" | custom-call | flops 120259084288 | bytes 16777216 | tf_op jit(solution)/shard_map/while/body/head/pallas_call | solution.py:261
  372.6 0.0 copy-start.18
  372.6 1.5 reduce_sum.186
  374.1 1.4 reduce_sum.185
  376.7 2.1 fusion.118
  378.8 2.3 fusion.119
  381.2 7.9 %convolution_add_fusion.9 = f32[2048,256]{1,0:T(8,128)} fusion(f32[2048,256]{1,0:T(8,128)} %get-tuple-element.493, bf16[1792,2048]{1,0:T(8,128)(2,1)} %copy-done.25, f32[1792,256]{1,0:T(8,128)S(1)} %fusion.119), kind=kOutput, calls=%fused_computation.31.clone.1 | convolution fusion | flops 1880031232 | bytes 13369344 | tf_op jit(solution)/shard_map/while/body/dot_general | solution.py:326
  389.0 12.6 %fusion.120 = (bf16[1792,2048]{1,0:T(8,128)(2,1)S(1)}, bf16[1792,2048]{1,0:T(8,128)(2,1)}) fusion(bf16[1792,2048]{1,0:T(8,128)(2,1)} %copy-done.5, bf16[1792,2048]{1,0:T(8,128)(2,1)} %get-tuple-element.459, bf16[2048,256]{1,0:T(8,128)(2,1)S(1)} %copy-done.24, f32[1792,256]{1,0:T(8,128)S(1)} %fusion.119), kind=kOutput, calls=%fused_computation.17.clone.1 | convolution fusion | flops 1934557184 | bytes 32243712 | tf_op jit(solution)/shard_map/while/body/dot_general | solution.py:325
  401.6 5.3 fusion.121
  407.0 0.1 copy-done.4
  407.1 5.3 convolution_add_fusion.7
  412.4 4.5 fusion.122
  416.9 3.1 convolution_add_fusion.8
  420.1 1.3 copy-done.10
  421.4 4.8 add.247
  426.1 18.4 %scatter_custom_fusion.5 = f32[4096,256]{1,0:T(8,128)} fusion(f32[4096,256]{1,0:T(8,128)} %add.247, s32[1792]{0:T(1024)} %copy-done.19, f32[1792,256]{1,0:T(8,128)} %copy-done.7, f32[1792,256]{1,0:T(8,128)} %get-tuple-element.462, f32[1792]{0:T(1024)S(1)} %broadcast_multiply_fusion.5, f32[1792]{0:T(1024)S(1)} %copy-done.20, ...), kind=kCustom, calls=%fused_computation.49.clone.1 | custom fusion | flops 3670016 | bytes 8805120 | tf_op jit(solution)/shard_map/while/body/scatter-add | solution.py:377
  444.8 0.0 reduce-scatter.8.cloned.1.call-update
  444.8 0.0 reduce-scatter.4.cloned.1.call-start
  444.9 0.5 reduce-scatter.4.cloned.1.call-update
  445.4 0.0 reduce-scatter.6.cloned.1.call-start
  445.4 0.5 reduce-scatter.6.cloned.1.call-update
  446.0 23.7 %psum.7 = f32[]{:T(128)} all-reduce(f32[]{:T(128)} %get-tuple-element.541), channel_id=1, replica_groups=mesh['fsdp'=8] {'fsdp'}, use_global_device_ids=true, to_apply=%region_19.20 | all-reduce | flops 1 | bytes 8 | tf_op jit(solution)/shard_map/psum | solution.py:383
  469.7 9.2 %reduce-scatter.8.cloned.1.call-done = f32[256,256]{1,0:T(8,128)} async-done(((f32[2048,256]{1,0:T(8,128)}), f32[256,256]{1,0:T(8,128)}) %reduce-scatter.8.cloned.1.call-update) | async-done | bytes 262160 | tf_op jit(solution)/shard_map/reduce_scatter | solution.py:344
  478.8 36.2 %reduce-scatter.4.cloned.1.call-done = f32[32,2048]{1,0:T(8,128)} async-done(((f32[256,2048]{1,0:T(8,128)}), f32[32,2048]{1,0:T(8,128)}) %reduce-scatter.4.cloned.1.call-update) | async-done | bytes 262160 | tf_op jit(solution)/shard_map/reduce_scatter | solution.py:344
  515.1 36.2 %reduce-scatter.6.cloned.1.call-done = f32[32,2048]{1,0:T(8,128)} async-done(((f32[256,2048]{1,0:T(8,128)}), f32[32,2048]{1,0:T(8,128)}) %reduce-scatter.6.cloned.1.call-update) | async-done | bytes 262160 | tf_op jit(solution)/shard_map/reduce_scatter | solution.py:344
  (53 shorter events, 0.1 us)
Async XLA Ops:
  7.2 35.1 %all-gather.4.cloned.1.call-start = ((), (), s32[]{:S(2)}) async-start(), calls=%async_computation.3 | async-start | bytes 1179648 | tf_op jit(solution)/shard_map/all_gather | solution.py:341
  7.9 41.8 %all-gather.6.cloned.1.call-start = ((), (), s32[]{:S(2)}) async-start(), calls=%async_computation.4 | async-start | bytes 1179648 | tf_op jit(solution)/shard_map/all_gather | solution.py:341
  8.6 60.5 %all-gather.8.cloned.1.call-start = ((), (), s32[]{:S(2)}) async-start(), calls=%async_computation.5 | async-start | bytes 1179648 | tf_op jit(solution)/shard_map/all_gather | solution.py:341
  9.4 469.5 %reduce-scatter.8.cloned.1.call-start = ((), (), s32[]{:S(2)}) async-start(), calls=%async_computation.8 | async-start | bytes 2359296 | tf_op jit(solution)/shard_map/reduce_scatter | solution.py:344
  73.8 2.4 copy-start.2
  100.3 0.6 copy-start.19
  100.3 20.0 %copy-start.14 = (pred[1792]{0:T(1024)(128)(4,1)}, pred[1792]{0:T(1024)(128)(4,1)S(1)}, u32[]{:S(2)}) copy-start(pred[1792]{0:T(1024)(128)(4,1)S(1)} %get-tuple-element.447) | copy-start | bytes 5380 | tf_op jit(solution)/shard_map/while
  106.4 13.9 %copy-start = (bf16[1792,256]{1,0:T(8,128)(2,1)}, bf16[1792,256]{1,0:T(8,128)(2,1)S(1)}, u32[]{:S(2)}) copy-start(bf16[1792,256]{1,0:T(8,128)(2,1)S(1)} %gather_fusion) | copy-start | bytes 2752516 | tf_op jit(solution)/shard_map/while
  107.6 4.3 copy-start.12
  107.6 4.3 copy-start.21
  111.9 8.4 %copy-start.5 = (bf16[1792,2048]{1,0:T(8,128)(2,1)}, bf16[1792,2048]{1,0:T(8,128)(2,1)S(1)}, u32[]{:S(2)}) copy-start(bf16[1792,2048]{1,0:T(8,128)(2,1)S(1)} %convolution_convert_fusion.3) | copy-start | bytes 22020100 | tf_op jit(solution)/shard_map/while
  111.9 8.4 %copy-start.23 = (bf16[2048,256]{1,0:T(8,128)(2,1)S(1)}, bf16[2048,256]{1,0:T(8,128)(2,1)}, u32[]{:S(2)}) copy-start(bf16[2048,256]{1,0:T(8,128)(2,1)} %get-tuple-element.523) | copy-start | bytes 3145732 | tf_op jit(solution)/shard_map/while
  120.2 3.4 copy-start.25
  124.2 0.6 copy-start.16
  372.6 6.2 %copy-start.6 = (f32[7,256,256]{2,1,0:T(8,128)S(1)}, f32[7,256,256]{2,1,0:T(8,128)}, u32[]{:S(2)}) copy-start(f32[7,256,256]{2,1,0:T(8,128)} %get-tuple-element.457) | copy-start | bytes 5505028 | tf_op jit(solution)/shard_map/while
  372.6 6.2 %copy-start.17 = (f32[1792]{0:T(1024)S(1)}, f32[1792]{0:T(1024)}, u32[]{:S(2)}) copy-start(f32[1792]{0:T(1024)} %copy-done.16) | copy-start | bytes 21508 | tf_op jit(solution)/shard_map/while
  372.6 6.2 %copy-start.18 = (f32[1792]{0:T(1024)S(1)}, f32[1792]{0:T(1024)}, u32[]{:S(2)}) copy-start(f32[1792]{0:T(1024)} %get-tuple-element.458) | copy-start | bytes 21508 | tf_op jit(solution)/shard_map/while
  381.1 7.9 %copy-start.7 = (f32[1792,256]{1,0:T(8,128)}, f32[1792,256]{1,0:T(8,128)S(1)}, u32[]{:S(2)}) copy-start(f32[1792,256]{1,0:T(8,128)S(1)} %fusion.119) | copy-start | bytes 5505028 | tf_op jit(solution)/shard_map/while
  381.1 7.9 %copy-start.24 = (bf16[2048,256]{1,0:T(8,128)(2,1)S(1)}, bf16[2048,256]{1,0:T(8,128)(2,1)}, u32[]{:S(2)}) copy-start(bf16[2048,256]{1,0:T(8,128)(2,1)} %get-tuple-element.523) | copy-start | bytes 3145732 | tf_op jit(solution)/shard_map/while
  389.0 12.6 %copy-start.11 = (bf16[256,2048]{1,0:T(8,128)(2,1)S(1)}, bf16[256,2048]{1,0:T(8,128)(2,1)}, u32[]{:S(2)}) copy-start(bf16[256,2048]{1,0:T(8,128)(2,1)} %get-tuple-element.521) | copy-start | bytes 3145732 | tf_op jit(solution)/shard_map/while
  401.6 5.4 copy-start.1
  401.6 5.5 copy-start.4
  401.6 5.5 copy-start.13
  401.6 5.5 copy-start.15
  407.1 5.3 copy-start.22
  412.4 4.5 copy-start.9
  416.9 4.4 copy-start.8
  420.1 1.3 copy-start.10
  421.4 4.8 copy-start.20
  426.1 18.4 %copy-start.3 = (bf16[4096,256]{1,0:T(8,128)(2,1)S(1)}, bf16[4096,256]{1,0:T(8,128)(2,1)}, u32[]{:S(2)}) copy-start(bf16[4096,256]{1,0:T(8,128)(2,1)} %get-tuple-element.563) | copy-start | bytes 6291460 | tf_op jit(solution)/shard_map/while
  444.8 70.3 %reduce-scatter.4.cloned.1.call-start = ((), (), s32[]{:S(2)}) async-start(), calls=%async_computation.6 | async-start | bytes 2359296 | tf_op jit(solution)/shard_map/reduce_scatter | solution.py:344
  445.4 105.9 %reduce-scatter.6.cloned.1.call-start = ((), (), s32[]{:S(2)}) async-start(), calls=%async_computation.7 | async-start | bytes 2359296 | tf_op jit(solution)/shard_map/reduce_scatter | solution.py:344
Sparse Core Ops, SparseCore 0:
  9.8 20.3 all-gather.3
  32.0 17.6 all-gather.5
  51.6 17.5 all-gather.7
  444.9 33.8 reduce-scatter.7
  482.5 32.5 reduce-scatter.3
  518.7 32.5 reduce-scatter.5

commit v2 on v1

--- a/solution.py
+++ b/solution.py
@@ -302,35 +302,268 @@
     return (rows_wide * inv_rms * norm_gain).astype(jnp.bfloat16), inv_rms
 
 
-def rms_back(rows_wide, inv_rms, norm_gain, grad_out):
-    scaled_grad = grad_out * norm_gain
-    return inv_rms * (scaled_grad - rows_wide * (inv_rms * inv_rms) * jnp.mean(scaled_grad * rows_wide, axis=-1, keepdims=True))
-
-
 def mlp_forward(emb_rows, gain_mlp, gain_head, w_gate, w_up, w_down):
     emb_wide = emb_rows.astype(jnp.float32)
-    a_norm, inv_first = rms_scale(emb_wide, gain_mlp)
-    gate_wide = jnp.dot(a_norm, w_gate, preferred_element_type=jnp.float32).astype(jnp.bfloat16).astype(jnp.float32)
-    up_wide = jnp.dot(a_norm, w_up, preferred_element_type=jnp.float32).astype(jnp.bfloat16).astype(jnp.float32)
-    gate_sig = jax.nn.sigmoid(gate_wide)
-    act_rows = (gate_wide * gate_sig * up_wide).astype(jnp.bfloat16)
-    hid_wide = (emb_wide + jnp.dot(act_rows, w_down, preferred_element_type=jnp.float32)).astype(jnp.bfloat16).astype(jnp.float32)
-    h_norm, inv_second = rms_scale(hid_wide, gain_head)
-    return (emb_wide, inv_first, a_norm, gate_wide, up_wide, gate_sig, act_rows, hid_wide, inv_second), h_norm
-
-
-def mlp_backward(saved, d_hidden, gain_mlp, w_gate, w_up, w_down):
-    emb_wide, inv_first, a_norm, gate_wide, up_wide, gate_sig, act_rows = saved[:7]
-    hid_grad = d_hidden.astype(jnp.bfloat16)
-    d_act = lax.dot_general(hid_grad, w_down, ROW_CONTRACT, preferred_element_type=jnp.float32)
-    grad_down = lax.dot_general(act_rows, hid_grad, TOK_CONTRACT, preferred_element_type=jnp.float32)
-    d_up = (d_act * gate_wide * gate_sig).astype(jnp.bfloat16)
-    d_gate = (d_act * up_wide * gate_sig * (1.0 + gate_wide * (1.0 - gate_sig))).astype(jnp.bfloat16)
-    grad_gate = lax.dot_general(a_norm, d_gate, TOK_CONTRACT, preferred_element_type=jnp.float32)
-    grad_up = lax.dot_general(a_norm, d_up, TOK_CONTRACT, preferred_element_type=jnp.float32)
-    d_anorm = lax.dot_general(d_gate, w_gate, ROW_CONTRACT, preferred_element_type=jnp.float32) + lax.dot_general(d_up, w_up, ROW_CONTRACT, preferred_element_type=jnp.float32)
-    grad_x = d_hidden + rms_back(emb_wide, inv_first, gain_mlp, d_anorm)
-    return grad_x, grad_gate, grad_up, grad_down
+    a_norm, _ = rms_scale(emb_wide, gain_mlp)
+    gate = jnp.dot(a_norm, w_gate, preferred_element_type=jnp.float32).astype(jnp.bfloat16)
+    up = jnp.dot(a_norm, w_up, preferred_element_type=jnp.float32).astype(jnp.bfloat16)
+    gate_wide = gate.astype(jnp.float32)
+    act = (gate_wide * jax.nn.sigmoid(gate_wide) * up.astype(jnp.float32)).astype(jnp.bfloat16)
+    hid = (emb_wide + jnp.dot(act, w_down, preferred_element_type=jnp.float32)).astype(jnp.bfloat16)
+    h_norm, _ = rms_scale(hid.astype(jnp.float32), gain_head)
+    return (hid, gate, up, act), h_norm
+
+
+def back_kernel(groups, dhn_ref, x_hbm, hid_hbm, gate_hbm, up_hbm, act_hbm, gain1_ref, gain2_ref, w_gate_hbm, w_up_hbm, w_down_hbm, rows_ref, head_hbm, loss_ref,
+                loss_out, dtable_ref, dgate_ref, dup_ref, ddown_ref,
+                x_buf, hid_buf, gate_buf, up_buf, act_buf, w_gate, w_up, w_down, head_buf, dh_wide, dh_narrow, dh_t, a_t, da_acc, dp_buf, dq_buf, dx_parts, inv_buf,
+                down_acc, down_core, down_first, down_second, wide_acc, wide_core, wide_first, wide_second, loss_all,
+                in_sems, tile_sems, loss_send, loss_recv, core_send, core_recv, first_send, first_recv, second_send, second_recv):
+    me = lax.axis_index("fsdp")
+    core = me % 2
+    first_step = 2 + 2 * core
+    second_step = 4 - 2 * core
+    chunk_w = 512
+    chunks = w_gate.shape[1] // chunk_w
+    f32, bf16 = jnp.float32, jnp.bfloat16
+
+    whole = [(x_hbm, x_buf), (hid_hbm, hid_buf), (act_hbm, act_buf), (w_down_hbm, w_down), (w_gate_hbm, w_gate), (w_up_hbm, w_up), (head_hbm, head_buf)]
+    loads = [pltpu.make_async_copy(src, dst, in_sems.at[i]) for i, (src, dst) in enumerate(whole)]
+    tiles = [pltpu.make_async_copy(src, dst, tile_sems.at[i]) for i, (src, dst) in enumerate([(gate_hbm, gate_buf), (up_hbm, up_buf)])]
+    for load in loads[:4] + tiles + loads[4:]:
+        load.start()
+    meet_all(me)
+
+    def loss_copy(step):
+        return remote(loss_ref, loss_all.at[step], loss_send.at[step], loss_recv.at[step], peer_of(me, step))
+
+    for step in range(1, N_DEV):
+        loss_copy(step).start()
+
+    def piece(unit, step):
+        if isinstance(unit, int) and unit == 0:
+            return down_acc.at[peer_of(me, step)]
+        return wide_acc.at[unit - 1, peer_of(me, step)]
+
+    def core_copy(unit, pair):
+        target = down_core.at[pair] if unit == 0 else wide_core.at[unit - 1, pair]
+        return remote(piece(unit, 2 * pair + 1), target, core_send.at[unit, pair], core_recv.at[unit, pair], peer_of(me, 1))
+
+    def first_copy(unit, which):
+        target = down_first.at[which] if unit == 0 else wide_first.at[unit - 1, which]
+        return remote(piece(unit, first_step if which == 0 else 6), target, first_send.at[unit, which], first_recv.at[unit, which], peer_of(me, first_step))
+
+    def second_copy(unit):
+        target = down_second if unit == 0 else wide_second.at[unit - 1]
+        return remote(piece(unit, second_step), target, second_send.at[unit], second_recv.at[unit], peer_of(me, second_step))
+
+    def send_core(unit):
+        for pair in (1, 2, 3, 0):
+            core_copy(unit, pair).start()
+
+    def add_core(unit):
+        for pair in (3, 2, 1, 0):
+            core_copy(unit, pair).wait_recv()
+            dst = piece(unit, 2 * pair)
+            dst[...] = dst[...] + (down_core[pair] if unit == 0 else wide_core[unit - 1, pair])
+        first_copy(unit, 1).start()
+        first_copy(unit, 0).start()
+
+    def add_first(unit):
+        for which in (1, 0):
+            first_copy(unit, which).wait_recv()
+            dst = piece(unit, second_step if which == 1 else 0)
+            dst[...] = dst[...] + (down_first[which] if unit == 0 else wide_first[unit - 1, which])
+        second_copy(unit).start()
+
+    def add_second(unit):
+        second_copy(unit).wait_recv()
+        if unit == 0:
+            ddown_ref[...] = down_acc[me] + down_second[...]
+        else:
+            both = wide_acc[unit - 1, me] + wide_second[unit - 1]
+            cols = slice((unit - 1) * chunk_w, unit * chunk_w)
+            dgate_ref[:, cols] = both[0]
+            dup_ref[:, cols] = both[1]
+
+    loads[0].wait()
+    loads[1].wait()
+
+    @pl.loop(0, groups)
+    def _(group):
+        rows = pl.ds(pl.multiple_of(group * UNIT, UNIT), UNIT)
+        hid = hid_buf[rows, :].astype(f32)
+        inv_second = lax.rsqrt(jnp.mean(hid * hid, axis=-1, keepdims=True) + NORM_EPS)
+        scaled = dhn_ref[group] * gain2_ref[...]
+        d_hid = inv_second * (scaled - hid * (inv_second * inv_second) * jnp.mean(scaled * hid, axis=-1, keepdims=True))
+        dh_wide[rows, :] = d_hid
+        dh_narrow[rows, :] = d_hid.astype(bf16)
+        dh_t[:, rows] = d_hid.astype(bf16).astype(f32).T.astype(bf16)
+        emb = x_buf[rows, :].astype(f32)
+        inv_first = lax.rsqrt(jnp.mean(emb * emb, axis=-1, keepdims=True) + NORM_EPS)
+        a_norm = (emb * inv_first * gain1_ref[...]).astype(bf16)
+        a_t[:, rows] = a_norm.astype(f32).T.astype(bf16)
+        da_acc[rows, :] = jnp.zeros((UNIT, 256), f32)
+
+    loads[2].wait()
+
+    @pl.loop(0, N_DEV)
+    def _(dev):
+        cols = pl.ds(pl.multiple_of(dev * 256, 256), 256)
+        down_acc[dev] = jnp.dot(dh_t[...], act_buf[:, cols], preferred_element_type=f32).T
+
+    send_core(0)
+    loads[3].wait()
+    for tile in tiles:
+        tile.wait()
+    loads[4].wait()
+    loads[5].wait()
+    for chunk in range(chunks):
+        cols = slice(chunk * chunk_w, (chunk + 1) * chunk_w)
+
+        @pl.loop(0, groups)
+        def _(group):
+            rows = pl.ds(pl.multiple_of(group * UNIT, UNIT), UNIT)
+            d_act = lax.dot_general(dh_narrow[rows, :], w_down[cols, :], ROW_CONTRACT, preferred_element_type=f32)
+            gate = gate_buf[rows, cols].astype(f32)
+            up = up_buf[rows, cols].astype(f32)
+            sig = jax.nn.sigmoid(gate)
+            d_up = (d_act * gate * sig).astype(bf16)
+            d_gate = (d_act * up * sig * (1.0 + gate * (1.0 - sig))).astype(bf16)
+            dp_buf[rows, :] = d_gate
+            dq_buf[rows, :] = d_up
+            da_acc[rows, :] += lax.dot_general(d_gate, w_gate[:, cols], ROW_CONTRACT, preferred_element_type=f32) + lax.dot_general(d_up, w_up[:, cols], ROW_CONTRACT, preferred_element_type=f32)
+
+        grad_gate = jnp.dot(a_t[...], dp_buf[...], preferred_element_type=f32)
+        wide_acc[chunk, :, 0] = grad_gate.reshape(N_DEV, 32, chunk_w)
+        grad_up = jnp.dot(a_t[...], dq_buf[...], preferred_element_type=f32)
+        wide_acc[chunk, :, 1] = grad_up.reshape(N_DEV, 32, chunk_w)
+        send_core(chunk + 1)
+        add_core(chunk)
+        if chunk >= 1:
+            add_first(chunk - 1)
+
+    @pl.loop(0, groups)
+    def _(group):
+        rows = pl.ds(pl.multiple_of(group * UNIT, UNIT), UNIT)
+        emb = x_buf[rows, :].astype(f32)
+        inv_first = lax.rsqrt(jnp.mean(emb * emb, axis=-1, keepdims=True) + NORM_EPS)
+        scaled = da_acc[rows, :] * gain1_ref[...]
+        dx = dh_wide[rows, :] + inv_first * (scaled - emb * (inv_first * inv_first) * jnp.mean(scaled * emb, axis=-1, keepdims=True))
+        high = dx.astype(bf16)
+        rest = dx - high.astype(f32)
+        middle = rest.astype(bf16)
+        dx_parts[rows, 0:256] = high
+        dx_parts[rows, 256:512] = middle
+        dx_parts[rows, 512:768] = (rest - middle.astype(f32)).astype(bf16)
+
+    add_core(chunks)
+    add_first(chunks - 1)
+    loads[6].wait()
+    row_block = 512
+    blocks = head_buf.shape[0] // row_block
+    row_iota = lax.broadcasted_iota(jnp.int32, (row_block, UNIT), 0)
+
+    def scatter_block(block):
+        base = block * row_block
+        rows = pl.ds(pl.multiple_of(base, row_block), row_block)
+        picks = jnp.concatenate([jnp.where(row_iota == rows_ref[group] - base, 1.0, 0.0).astype(bf16) for group in range(groups)], axis=1)
+        parts = jnp.dot(picks, dx_parts[...], preferred_element_type=f32)
+        dtable_ref[rows, :] = head_buf[rows, :] + (parts[:, 0:256] + (parts[:, 256:512] + parts[:, 512:768]))
+
+    @pl.loop(0, blocks // 2)
+    def _(block):
+        scatter_block(block)
+
+    add_first(chunks)
+
+    @pl.loop(blocks // 2, blocks)
+    def _(block):
+        scatter_block(block)
+
+    total = loss_ref[...]
+    for step in range(1, N_DEV):
+        loss_copy(step).wait_recv()
+        total = total + loss_all[step]
+    loss_out[...] = total
+    for unit in range(chunks + 1):
+        add_second(unit)
+    for step in range(1, N_DEV):
+        loss_copy(step).wait_send()
+    for unit in range(chunks + 1):
+        for pair in range(4):
+            core_copy(unit, pair).wait_send()
+        first_copy(unit, 0).wait_send()
+        first_copy(unit, 1).wait_send()
+        second_copy(unit).wait_send()
+
+
+def back_call(d_hnorm, x_rows, hid, gate, up, act, gain_mlp, gain_head, w_gate, w_up, w_down, row_id, head_grad, loss_part):
+    groups, _, width = d_hnorm.shape
+    slots, wide = gate.shape
+    vocab = head_grad.shape[0]
+    chunks = wide // 512
+    units = chunks + 1
+    f32, bf16 = jnp.float32, jnp.bfloat16
+    dma = pltpu.SemaphoreType.DMA
+    vmem = pl.BlockSpec(memory_space=pltpu.VMEM)
+    hbm = pl.BlockSpec(memory_space=pl.ANY)
+    piece_d = (wide // N_DEV, width)
+    piece_w = (2, width // N_DEV, 512)
+    return pl.pallas_call(
+        functools.partial(back_kernel, groups),
+        out_shape=(
+            jax.ShapeDtypeStruct((8, 128), f32),
+            jax.ShapeDtypeStruct((vocab, width), f32),
+            jax.ShapeDtypeStruct((width // N_DEV, wide), f32),
+            jax.ShapeDtypeStruct((width // N_DEV, wide), f32),
+            jax.ShapeDtypeStruct(piece_d, f32),
+        ),
+        in_specs=[vmem, hbm, hbm, hbm, hbm, hbm, vmem, vmem, hbm, hbm, hbm, vmem, hbm, vmem],
+        out_specs=(vmem,) * 5,
+        scratch_shapes=[
+            pltpu.VMEM((slots, width), bf16),
+            pltpu.VMEM((slots, width), bf16),
+            pltpu.VMEM((slots, wide), bf16),
+            pltpu.VMEM((slots, wide), bf16),
+            pltpu.VMEM((slots, wide), bf16),
+            pltpu.VMEM((width, wide), bf16),
+            pltpu.VMEM((width, wide), bf16),
+            pltpu.VMEM((wide, width), bf16),
+            pltpu.VMEM((vocab, width), f32),
+            pltpu.VMEM((slots, width), f32),
+            pltpu.VMEM((slots, width), bf16),
+            pltpu.VMEM((width, slots), bf16),
+            pltpu.VMEM((width, slots), bf16),
+            pltpu.VMEM((slots, width), f32),
+            pltpu.VMEM((slots, 512), bf16),
+            pltpu.VMEM((slots, 512), bf16),
+            pltpu.VMEM((slots, 3 * width), bf16),
+            pltpu.VMEM((8, 128), f32),
+            pltpu.VMEM((N_DEV,) + piece_d, f32),
+            pltpu.VMEM((4,) + piece_d, f32),
+            pltpu.VMEM((2,) + piece_d, f32),
+            pltpu.VMEM(piece_d, f32),
+            pltpu.VMEM((chunks, N_DEV) + piece_w, f32),
+            pltpu.VMEM((chunks, 4) + piece_w, f32),
+            pltpu.VMEM((chunks, 2) + piece_w, f32),
+            pltpu.VMEM((chunks,) + piece_w, f32),
+            pltpu.VMEM((N_DEV, 8, 128), f32),
+            dma((7,)),
+            dma((2,)),
+            dma((N_DEV,)),
+            dma((N_DEV,)),
+            dma((units, 4)),
+            dma((units, 4)),
+            dma((units, 2)),
+            dma((units, 2)),
+            dma((units,)),
+            dma((units,)),
+        ],
+        compiler_params=pltpu.CompilerParams(collective_id=2, has_side_effects=True, vmem_limit_bytes=VMEM_MAX),
+        cost_estimate=pl.CostEstimate(flops=16 * slots * wide * width, bytes_accessed=6 * slots * wide, transcendentals=slots * wide),
+        name="back",
+    )(d_hnorm, x_rows, hid, gate, up, act, gain_mlp.reshape(1, width), gain_head.reshape(1, width), w_gate, w_up, w_down, row_id, head_grad, loss_part)
 
 
 GROUPS = 7
@@ -339,9 +572,6 @@
 def solution(mesh):
     def gather_rows(row_shard):
         return lax.all_gather(row_shard, "fsdp", axis=0, tiled=True)
-
-    def scatter_rows(full_rows):
-        return lax.psum_scatter(full_rows, "fsdp", scatter_dimension=0, tiled=True)
 
     def device_step(tok_ids, tok_labels, loss_mask, table_shard, gain_mlp, gain_head, gate_shard, up_shard, down_shard):
         me = lax.axis_index("fsdp")
@@ -364,23 +594,28 @@
         norm_rows = jnp.zeros((8, 128), jnp.float32).at[0].set(jnp.log2(count)).at[1].set(1.0 / count)
         table_t = table_shard.T
 
-        def one_round(state):
-            turn, loss, g_table, g_gate, g_up, g_down = state
+        def one_round(turn):
             mine = lax.dynamic_slice(packed, (turn * slots,), (slots,))
             valid = mine != last
             row_id = jnp.where(valid, mine // vocab_all, 0)
             label = jnp.where(valid, mine % vocab_all, -1)
-            saved, h_norm = mlp_forward(jnp.take(table_shard, row_id, axis=0), gain_mlp, gain_head, gate_full, up_full, down_full)
+            x_rows = jnp.take(table_shard, row_id, axis=0)
+            (hid, gate, up, act), h_norm = mlp_forward(x_rows, gain_mlp, gain_head, gate_full, up_full, down_full)
             d_hnorm, head_grad, lse, picked = head_call(h_norm.reshape(GROUPS, UNIT, width), label.reshape(GROUPS, 1, UNIT), norm_rows, table_shard, table_t, GROUPS)
-            d_hidden = rms_back(saved[7], saved[8], gain_head, d_hnorm.reshape(slots, width))
-            grad_x, grad_gate, grad_up, grad_down = mlp_backward(saved, d_hidden, gain_mlp, gate_full, up_full, down_full)
-            in_grad = jax.ops.segment_sum(grad_x, row_id, num_segments=vocab)
             part = (jnp.sum(lse) * LN2 - jnp.sum(picked)) / count
-            return (turn + 1, loss + part, g_table + head_grad + in_grad, g_gate + grad_gate, g_up + grad_up, g_down + grad_down)
-
-        zeros = (jnp.int32(0), jnp.float32(0), jnp.zeros((vocab, width), jnp.float32), jnp.zeros(gate_full.shape, jnp.float32), jnp.zeros(up_full.shape, jnp.float32), jnp.zeros(down_full.shape, jnp.float32))
-        _, loss, g_table, g_gate, g_up, g_down = lax.while_loop(lambda state: state[0] < rounds, one_round, zeros)
-        return (lax.psum(loss, "fsdp"), g_table, scatter_rows(g_gate), scatter_rows(g_up), scatter_rows(g_down))
+            loss_part = jnp.broadcast_to(part, (8, 128))
+            return back_call(d_hnorm, x_rows, hid, gate, up, act, gain_mlp, gain_head, gate_full, up_full, down_full, row_id.reshape(GROUPS, 1, UNIT), head_grad, loss_part)
+
+        def more_rounds(sums):
+            def step(state):
+                extra = one_round(state[0])
+                return (state[0] + 1, tuple(old + new for old, new in zip(state[1], extra)))
+
+            return lax.while_loop(lambda state: state[0] < rounds, step, (jnp.int32(1), tuple(sums)))[1]
+
+        sums = lax.cond(rounds > 1, more_rounds, tuple, one_round(jnp.int32(0)))
+        loss, g_table, g_gate, g_up, g_down = sums
+        return (loss[0, 0], g_table, g_gate, g_up, g_down)
 
     row_spec = P("fsdp", None)
     tok_spec = P("fsdp")

time: 566 us -> 409 us (0.72)
  waiting for transfers between devices: 112 us -> 7.11 us
  Pallas kernels: 254 us -> 313 us
  matrix products: 54.7 us -> 22.4 us
  other arithmetic: 48.1 us -> 16.5 us
  blocking collectives: 23.7 us -> 0 us
  loops' own time: 24.1 us -> 1.72 us
    reduce_scatter x3 -> x0, waiting for transfers between devices: 81.6 us -> none  [scatter_rows(): return lax.psum_scatter(full_rows, 'fsdp', scatter_dimension=0, tiled=True)]
    pallas_call x0 -> x1, Pallas kernels: none -> 58.9 us  [back_call(): pl.pallas_call(functools.partial(back_kernel, groups), out_shape=(jax.Sha...]
    dot_general x7 -> x1, matrix products: 42.1 us -> 5.58 us  [mlp_forward(): jnp.dot(act, w_down, preferred_element_type=jnp.float32)]
    psum x1 -> x0, blocking collectives: 23.7 us -> none  [device_step(): lax.psum(loss, 'fsdp')]
    another operation x1, loops' own time: 24.1 us -> 1.72 us  [device_step(): sums = lax.cond(rounds > 1, more_rounds, tuple, one_round(jnp.int32(0)))]
    all_gather x3, waiting for transfers between devices: 26.9 us -> 5.06 us  [gather_rows(): return lax.all_gather(row_shard, 'fsdp', axis=0, tiled=True)]
    scatter-add x1 -> x0, other arithmetic: 18.4 us -> none  [one_round(): in_grad = jax.ops.segment_sum(grad_x, row_id, num_segments=vocab)]
    unnamed x3 -> x25, local copies, waits for them, and re-layouts: 4.28 us -> 11.7 us
  transfers between devices with their start and end apart: 6 -> 3, of which waited for: 5 -> 1; matrix products, arithmetic and copies ran while one was open for 3% -> 10% of each run, Pallas kernels for 2% -> 2%
where the time goes in v2:
time: 409 us; the launch traced here: 402 us
  Pallas kernels  313 us (77%)
  matrix products  22.4 us (5%)
  between operations  21.3 us (5%)
  local copies, waits for them, and re-layouts  20.4 us (5%)
  other arithmetic  16.5 us (4%)
  waiting for transfers between devices  7.11 us (2%)
    pallas_call x1, Pallas kernels, head_call(): pl.pallas_call(functools.partial(head_kernel, groups, vocab), out_shape=(...  245 us
    pallas_call x1, Pallas kernels, back_call(): pl.pallas_call(functools.partial(back_kernel, groups), out_shape=(jax.Sha...  58.9 us
    unnamed x25, local copies, waits for them, and re-layouts  11.7 us
    dot_general x1, matrix products, mlp_forward(): jnp.dot(a_norm, w_up, preferred_element_type=jnp.float32)  10.5 us
    pallas_call x1, Pallas kernels, gather_tokens(): pl.pallas_call(tokens_kernel, out_shape=jax.ShapeDtypeStruct((N_DEV,) + t...  8.46 us
  transfers between devices with their start and end apart: 3, of which 1 were waited for; matrix products, arithmetic and copies ran while one was open for 10% of the time, Pallas kernels for 2%

profile of v2, /device:TPU:0, one launch (start us, length us, event | category | flops | bytes accessed | tf_op | source)
XLA Modules:
  0.0 402.3 jit_solution(5261799000453389127)
XLA Ops:
  7.2 0.0 copy-start
  7.2 0.0 all-gather.4.cloned.1.call-start
  7.2 0.7 all-gather.4.cloned.1.call-update
  7.9 0.0 all-gather.6.cloned.1.call-start
  8.0 0.7 all-gather.6.cloned.1.call-update
  8.7 0.0 all-gather.8.cloned.1.call-start
  8.7 0.7 all-gather.8.cloned.1.call-update
  9.4 1.3 pad_add_fusion.tok_hbm
  10.7 8.5 %gather_tokens.1 = s32[8,3,16,128]{3,2,1,0:T(8,128)} custom-call(s32[3,16,128]{2,1,0:T(8,128)} %pad_add_fusion.tok_hbm), custom_call_target="tpu_custom_call" | custom-call | tf_op jit(solution)/shard_map/gather_tokens/pallas_call | solution.py:61
  19.2 0.9 broadcast_compare_fusion
  20.1 1.8 slice_reduce_fusion
  27.0 0.1 add_select_fusion.4
  27.0 7.7 %sort.15 = (s32[16384]{0:T(1024)S(1)}, s32[16384]{0:T(1024)}) sort(s32[16384]{0:T(1024)S(1)} %add_select_fusion.4, s32[16384]{0:T(1024)S(1)} %iota.3), dimensions={0}, to_apply=%region_8.9 | sort | flops 229376 | bytes 262144 | tf_op jit(solution)/shard_map/jit(sort)/sort | solution.py:591
  34.8 0.0 copy-start.14
  35.6 0.6 select_n.170.rows_ref
  36.2 0.6 copy.15.lab_hbm
  36.8 0.0 copy-done.14
  36.8 4.1 %copy.14 = bf16[4096,256]{0,1:T(8,128)(2,1)} copy(bf16[4096,256]{1,0:T(8,128)(2,1)} %table_ref.1) | data formatting | bytes 4194304 | tf_op args[3]
  40.9 0.0 copy-done
  40.9 0.0 copy-start.12
  40.9 5.5 %gather_fusion.1 = bf16[1792,256]{1,0:T(8,128)(2,1)S(1)} fusion(bf16[4096,256]{1,0:T(8,128)(2,1)S(1)} %copy-done, s32[2048]{0:T(1024)S(1)} %pad_clamp_fusion.1), kind=kCustom, calls=%fused_computation.1 | custom fusion | bytes 1842176 | tf_op jit(solution)/shard_map/jit(_take)/gather | solution.py:602
  46.4 0.7 fusion.27
  47.1 0.0 copy-start.8
  47.2 0.1 scatter.13
  47.2 0.2 scatter.14.norm_ref
  47.4 0.0 copy-start.17
  47.4 0.0 all-gather.4.cloned.1.call-done.w_gate_hbm
  47.4 0.0 copy-done.12
  47.5 6.3 %convolution_convert_fusion.3.gate_hbm = bf16[1792,2048]{1,0:T(8,128)(2,1)} fusion(bf16[256,2048]{1,0:T(8,128)(2,1)} %all-gather.4.cloned.1.call-done.w_gate_hbm, bf16[1792,256]{1,0:T(8,128)(2,1)S(1)} %get-tuple-element.410.x_hbm, f32[256]{0:T(256)S(1)} %copy-done.12, f32[1792]{0:T(1024)S(1)} %add_rsqrt_fusion.3), kind=kOutput, calls=%fused_computation.48 | convolution fusion | flops 1884553216 | bytes 9314304 | tf_op jit(solution)/shard_map/dot_general | solution.py:308
  53.8 0.0 copy-done.17
  53.8 0.0 all-gather.6.cloned.1.call-done.w_up_hbm
  53.8 10.5 %fusion.22 = (bf16[1792,2048]{1,0:T(8,128)(2,1)}, bf16[1792,2048]{1,0:T(8,128)(2,1)}) fusion(bf16[1792,2048]{1,0:T(8,128)(2,1)} %convolution_convert_fusion.3.gate_hbm, bf16[256,2048]{1,0:T(8,128)(2,1)} %all-gather.6.cloned.1.call-done.w_up_hbm, bf16[1792,256]{1,0:T(8,128)(2,1)S(1)} %get-tuple-element.410.x_hbm, f32[256]{0:T(256)S(1)} %copy-done.12, ...), kind=kOutput, calls=%fused_computation.46 | convolution fusion | flops 1913913344 | bytes 23994368 | tf_op jit(solution)/shard_map/dot_general | solution.py:309
  64.2 5.0 %all-gather.8.cloned.1.call-done.w_down_hbm = bf16[2048,256]{1,0:T(8,128)(2,1)} async-done(((bf16[256,256]{1,0:T(8,128)(2,1)}), bf16[2048,256]{1,0:T(8,128)(2,1)}) %all-gather.8.cloned.1.call-update) | async-done | bytes 1048592 | tf_op jit(solution)/shard_map/all_gather | solution.py:574
  69.3 0.0 copy-done.8
  69.3 0.0 copy-start.15
  69.3 5.6 %fusion.24 = (f32[1792]{0:T(1024)S(1)}, bf16[1792,256]{1,0:T(8,128)(2,1)S(1)}) fusion(bf16[1792,2048]{1,0:T(8,128)(2,1)} %get-tuple-element.421.act_hbm, bf16[2048,256]{1,0:T(8,128)(2,1)} %all-gather.8.cloned.1.call-done.w_down_hbm, bf16[1792,256]{1,0:T(8,128)(2,1)S(1)} %get-tuple-element.410.x_hbm), kind=kOutput, calls=%fused_computation.55 | convolution fusion | flops 1881798912 | bytes 10230784 | tf_op jit(solution)/shard_map/dot_general | solution.py:312
  74.9 0.0 copy-start.9
  74.9 0.9 copy-done.9
  75.8 0.0 copy-done.15
  75.8 1.2 fusion.26
  77.0 245.4 %head.5 = (f32[7,256,256]{2,1,0:T(8,128)}, f32[4096,256]{1,0:T(8,128)}, f32[7,1,256]{2,1,0:T(1,128)}, f32[8,512]{1,0:T(8,128)}) custom-call(bf16[7,256,256]{2,1,0:T(8,128)(2,1)} %bitcast.43, s32[7,1,256]{2,1,0:T(1,128)} %copy.15.lab_hbm, f32[8,128]{1,0:T(8,128)} %copy-done.17, bf16[4096,256]{1,0:T(8,128)(2,1)} %table_ref.1, bf16[256,4096]{1,0:T(8,128)(2,1)} %bitcast.41), custom_call_target="tpu_custom_call" | custom-call | flops 120259084288 | bytes 16777216 | tf_op jit(solution)/shard_map/head/pallas_call | solution.py:261
  322.4 1.3 reduce_sum.177
  323.8 1.3 reduce_sum.176
  326.4 0.6 broadcast_in_dim.90.loss_ref
  327.0 58.9 %back.5 = (f32[8,128]{1,0:T(8,128)}, f32[4096,256]{1,0:T(8,128)}, f32[32,2048]{1,0:T(8,128)}, f32[32,2048]{1,0:T(8,128)}, f32[256,256]{1,0:T(8,128)}) custom-call(f32[7,256,256]{2,1,0:T(8,128)} %get-tuple-element.339.dhn_ref, bf16[1792,256]{1,0:T(8,128)(2,1)} %copy-done.8, bf16[1792,256]{1,0:T(8,128)(2,1)} %copy-done.9, ...), custom_call_target="tpu_custom_call" | custom-call | flops 15032385536 | bytes 22020096 | tf_op jit(solution)/shard_map/back/pallas_call | solution.py:513
  386.0 2.9 conditional.1
  386.0 1.2 slice.71
  388.9 0.0 copy-start.5
  388.9 0.0 copy-start.6
  388.9 0.0 copy-start.7
  388.9 4.5 %copy.49 = f32[4096,256]{1,0:T(8,128)} copy(f32[4096,256]{1,0:T(8,128)} %get-tuple-element.654) | data formatting | bytes 8388608
  393.4 0.0 copy-done.5
  393.4 0.7 copy.50
  394.1 0.0 copy-done.6
  394.1 0.7 copy.51
  394.8 0.0 copy-done.7
  394.8 0.7 copy.52
  (10 shorter events, 0.1 us)
Async XLA Ops:
  7.2 33.7 %copy-start = (bf16[4096,256]{1,0:T(8,128)(2,1)S(1)}, bf16[4096,256]{1,0:T(8,128)(2,1)}, u32[]{:S(2)}) copy-start(bf16[4096,256]{1,0:T(8,128)(2,1)} %table_ref.1) | copy-start | bytes 6291460
  7.2 40.3 %all-gather.4.cloned.1.call-start = ((), (), s32[]{:S(2)}) async-start(), calls=%async_computation | async-start | bytes 1179648 | tf_op jit(solution)/shard_map/all_gather | solution.py:574
  7.9 45.9 %all-gather.6.cloned.1.call-start = ((), (), s32[]{:S(2)}) async-start(), calls=%async_computation.1 | async-start | bytes 1179648 | tf_op jit(solution)/shard_map/all_gather | solution.py:574
  8.7 60.6 %all-gather.8.cloned.1.call-start = ((), (), s32[]{:S(2)}) async-start(), calls=%async_computation.2 | async-start | bytes 1179648 | tf_op jit(solution)/shard_map/all_gather | solution.py:574
  34.8 2.0 copy-start.14
  40.9 6.6 %copy-start.12 = (f32[256]{0:T(256)S(1)}, f32[256]{0:T(256)}, u32[]{:S(2)}) copy-start(f32[256]{0:T(256)} %param.21) | copy-start | bytes 3076
  47.1 22.2 %copy-start.8 = (bf16[1792,256]{1,0:T(8,128)(2,1)}, bf16[1792,256]{1,0:T(8,128)(2,1)S(1)}, u32[]{:S(2)}) copy-start(bf16[1792,256]{1,0:T(8,128)(2,1)S(1)} %get-tuple-element.410.x_hbm) | copy-start | bytes 2752516
  47.4 6.4 %copy-start.17 = (f32[8,128]{1,0:T(8,128)}, f32[8,128]{1,0:T(8,128)S(1)}, u32[]{:S(2)}) copy-start(f32[8,128]{1,0:T(8,128)S(1)} %scatter.14.norm_ref) | copy-start | bytes 12292
  69.3 6.5 %copy-start.15 = (f32[256]{0:T(256)S(1)}, f32[256]{0:T(256)}, u32[]{:S(2)}) copy-start(f32[256]{0:T(256)} %param.22) | copy-start | bytes 3076
  74.9 0.9 copy-start.9
  388.9 4.6 %copy-start.5 = (f32[32,2048]{1,0:T(8,128)S(1)}, f32[32,2048]{1,0:T(8,128)}, u32[]{:S(2)}) copy-start(f32[32,2048]{1,0:T(8,128)} %get-tuple-element.655) | copy-start | bytes 786436
  388.9 5.3 %copy-start.6 = (f32[32,2048]{1,0:T(8,128)S(1)}, f32[32,2048]{1,0:T(8,128)}, u32[]{:S(2)}) copy-start(f32[32,2048]{1,0:T(8,128)} %get-tuple-element.656) | copy-start | bytes 786436
  388.9 6.0 %copy-start.7 = (f32[256,256]{1,0:T(8,128)S(1)}, f32[256,256]{1,0:T(8,128)}, u32[]{:S(2)}) copy-start(f32[256,256]{1,0:T(8,128)} %get-tuple-element.657) | copy-start | bytes 786436
Sparse Core Ops, SparseCore 0:
  9.8 20.3 all-gather.3
  32.0 17.7 all-gather.5
  51.7 17.5 all-gather.7

commit v3 on v2

--- a/solution.py
+++ b/solution.py
@@ -16,8 +16,10 @@
 LN2 = math.log(2.0)
 N_DEV = 8
 UNIT = 256
-V_CHUNK = 512
+V_CHUNK = 1024
 VMEM_MAX = 67_043_328
+LAST_KEY = 2**31 - 1
+WIDE_CHUNK = 1024
 
 
 def peer_of(me, step):
@@ -42,31 +44,69 @@
     return pltpu.make_async_remote_copy(src_ref=src, dst_ref=dst, send_sem=send_sem, recv_sem=recv_sem, device_id=(target,), device_id_type=MESH)
 
 
-def tokens_kernel(tok_hbm, all_ref, local_sem, send_sems, recv_sems):
+def tokens_kernel(ids_hbm, labels_hbm, mask_hbm, table_hbm, packed_ref, info_ref, table_t_ref, every, table_buf, local_sems, send_sems, recv_sems):
     me = lax.axis_index("fsdp")
-    own = pltpu.make_async_copy(tok_hbm, all_ref.at[0], local_sem)
-    own.start()
+    vocab = table_buf.shape[0]
+    own = [pltpu.make_async_copy(src, every.at[which, 0], local_sems.at[which]) for which, src in enumerate((ids_hbm, labels_hbm, mask_hbm))]
+    table_copy = pltpu.make_async_copy(table_hbm, table_buf, local_sems.at[3])
+    for copy in own + [table_copy]:
+        copy.start()
     meet_all(me)
-    own.wait()
+    for copy in own:
+        copy.wait()
     copies = []
     for step in range(1, N_DEV):
-        copy = remote(all_ref.at[0], all_ref.at[step], send_sems.at[step], recv_sems.at[step], peer_of(me, step))
+        copy = remote(every.at[:, 0], every.at[:, step], send_sems.at[step], recv_sems.at[step], peer_of(me, step))
         copy.start()
         copies.append(copy)
+    table_copy.wait()
+
+    @pl.loop(0, vocab // 512)
+    def _(block):
+        rows = pl.ds(pl.multiple_of(block * 512, 512), 512)
+        table_t_ref[:, rows] = table_buf[rows, :].astype(jnp.float32).T.astype(jnp.bfloat16)
+
     for copy in copies:
         copy.wait()
-
-
-def gather_tokens(tok_block):
+    ids, labels, mask = every[0], every[1], every[2]
+    local = ids - me * vocab
+    mine = (local >= 0) & (local < vocab) & (mask != 0)
+    packed_ref[...] = jnp.where(mine, local * (vocab * N_DEV) + labels, LAST_KEY)
+    weight = mask.astype(jnp.float32)
+
+    def total(rows):
+        return jnp.sum(jnp.sum(jnp.sum(rows, axis=0), axis=0, keepdims=True), axis=1, keepdims=True)
+
+    count = total(weight)
+    load = jnp.zeros((1, 1), jnp.float32)
+    for dev in range(N_DEV):
+        here = (ids >= dev * vocab) & (ids < (dev + 1) * vocab)
+        load = jnp.maximum(load, total(jnp.where(here, weight, 0.0)))
+    info_ref[0:1, :] = jnp.broadcast_to(jnp.log2(count), (1, 128))
+    info_ref[1:2, :] = jnp.broadcast_to(1.0 / count, (1, 128))
+    info_ref[2:3, :] = jnp.broadcast_to(load, (1, 128))
+    info_ref[3:8, :] = jnp.zeros((5, 128), jnp.float32)
+
+
+def gather_tokens(ids, labels, mask, table):
+    rows = (ids.shape[0] // 128, 128)
+    vocab, width = table.shape
+    dma = pltpu.SemaphoreType.DMA
+    vmem = pl.BlockSpec(memory_space=pltpu.VMEM)
+    hbm = pl.BlockSpec(memory_space=pl.ANY)
     return pl.pallas_call(
         tokens_kernel,
-        out_shape=jax.ShapeDtypeStruct((N_DEV,) + tok_block.shape, tok_block.dtype),
-        in_specs=[pl.BlockSpec(memory_space=pl.ANY)],
-        out_specs=pl.BlockSpec(memory_space=pltpu.VMEM),
-        scratch_shapes=[pltpu.SemaphoreType.DMA, pltpu.SemaphoreType.DMA((N_DEV,)), pltpu.SemaphoreType.DMA((N_DEV,))],
+        out_shape=(
+            jax.ShapeDtypeStruct((N_DEV,) + rows, jnp.int32),
+            jax.ShapeDtypeStruct((8, 128), jnp.float32),
+            jax.ShapeDtypeStruct((width, vocab), jnp.bfloat16),
+        ),
+        in_specs=[hbm] * 4,
+        out_specs=(vmem,) * 3,
+        scratch_shapes=[pltpu.VMEM((3, N_DEV) + rows, jnp.int32), pltpu.VMEM((vocab, width), jnp.bfloat16), dma((4,)), dma((N_DEV,)), dma((N_DEV,))],
         compiler_params=pltpu.CompilerParams(collective_id=0, has_side_effects=True),
         name="gather_tokens",
-    )(tok_block)
+    )(ids.reshape(rows), labels.reshape(rows), mask.reshape(rows), table)
 
 
 def head_kernel(groups, vocab, hn_hbm, lab_hbm, norm_ref, table_ref, table_t_ref, dhn_ref, dtable_ref, lse_ref, pick_ref,
@@ -120,10 +160,17 @@
     def _(group):
         @pl.loop(0, 4)
         def _(pair):
-            @pl.when(pair > 0)
-            def _():
+            def pass_on(pair):
                 own_send(2 * pair, group).wait_recv()
                 forward(2 * pair, group).start()
+
+            @pl.when((pair == 1) & (group == 0))
+            def _():
+                pass_on(1)
+
+            @pl.when((pair < 3) & (pair + group > 0))
+            def _():
+                pass_on(pair + 1)
 
             @pl.when(pair == 0)
             def _():
@@ -199,13 +246,18 @@
 
             tile = hn_all[group, pl.ds(2 * pair, 2)].reshape(pair_rows, 256)
             local_label = label - me * vocab
+            sub_row = lax.broadcasted_iota(jnp.int32, (8, pair_rows), 0)
+            tile_row = jnp.where(local_label % 8 == sub_row, local_label // 8, -1)
+            block_row = lax.broadcasted_iota(jnp.int32, (V_CHUNK // 8, 8, pair_rows), 0)
             picked = jnp.zeros((8, pair_rows), jnp.float32)
             for chunk in range(chunks):
                 logits = lax.dot_general(table_rows(chunk), tile, ROW_CONTRACT, preferred_element_type=jnp.float32)
-                is_label = row_iota == (local_label - chunk * V_CHUNK)
-                picked += jnp.sum(jnp.where(is_label, logits, 0.0).reshape(V_CHUNK // 8, 8, pair_rows), axis=0)
-                prob = jnp.exp2(logits * LOG2E - shift)
-                d_logits = jnp.where(is_label, prob - inv_n, prob).astype(jnp.bfloat16)
+                logits = logits.reshape(V_CHUNK // 8, 8, pair_rows)
+                is_label = block_row == (tile_row - chunk * (V_CHUNK // 8))[None]
+                for row in range(V_CHUNK // 8):
+                    picked = jnp.where(is_label[row], logits[row], picked)
+                prob = jnp.exp2(logits * LOG2E - shift[None])
+                d_logits = jnp.where(is_label, prob - inv_n[None], prob).reshape(V_CHUNK, pair_rows).astype(jnp.bfloat16)
                 rows = pl.ds(chunk * V_CHUNK, V_CHUNK)
                 dtable_ref[rows, :] += jnp.dot(d_logits, tile, preferred_element_type=jnp.float32)
                 d_part = jnp.dot(table_t_ref[:, rows], d_logits, preferred_element_type=jnp.float32)
@@ -251,7 +303,7 @@
         label_send(step).wait_send()
 
 
-def head_call(h_norm, labels, norm_rows, table, table_t, groups):
+def head_call(h_norm, labels, norm_rows, table, table_t, groups, variant=0):
     vocab = table.shape[0]
     dma = pltpu.SemaphoreType.DMA
     vmem = pl.BlockSpec(memory_space=pltpu.VMEM)
@@ -291,7 +343,7 @@
             dma((groups, 4)),
             dma((groups, 4)),
         ],
-        compiler_params=pltpu.CompilerParams(collective_id=1, has_side_effects=True, vmem_limit_bytes=VMEM_MAX),
+        compiler_params=pltpu.CompilerParams(collective_id=1 + 2 * variant, has_side_effects=True, vmem_limit_bytes=VMEM_MAX),
         cost_estimate=pl.CostEstimate(flops=8 * tokens * vocab * 256, bytes_accessed=16 * vocab * 256, transcendentals=2 * tokens * vocab),
         name="head",
     )(h_norm, labels, norm_rows, table, table_t)
@@ -302,43 +354,97 @@
     return (rows_wide * inv_rms * norm_gain).astype(jnp.bfloat16), inv_rms
 
 
-def mlp_forward(emb_rows, gain_mlp, gain_head, w_gate, w_up, w_down):
-    emb_wide = emb_rows.astype(jnp.float32)
-    a_norm, _ = rms_scale(emb_wide, gain_mlp)
-    gate = jnp.dot(a_norm, w_gate, preferred_element_type=jnp.float32).astype(jnp.bfloat16)
-    up = jnp.dot(a_norm, w_up, preferred_element_type=jnp.float32).astype(jnp.bfloat16)
-    gate_wide = gate.astype(jnp.float32)
-    act = (gate_wide * jax.nn.sigmoid(gate_wide) * up.astype(jnp.float32)).astype(jnp.bfloat16)
-    hid = (emb_wide + jnp.dot(act, w_down, preferred_element_type=jnp.float32)).astype(jnp.bfloat16)
-    h_norm, _ = rms_scale(hid.astype(jnp.float32), gain_head)
-    return (hid, gate, up, act), h_norm
-
-
-def back_kernel(groups, dhn_ref, x_hbm, hid_hbm, gate_hbm, up_hbm, act_hbm, gain1_ref, gain2_ref, w_gate_hbm, w_up_hbm, w_down_hbm, rows_ref, head_hbm, loss_ref,
+def forward_kernel(*refs):
+    wide_slots, down_slots = refs[:N_DEV], refs[N_DEV : 2 * N_DEV]
+    x_ref, gain1_ref, gain2_ref, hid_ref, gate_ref, up_ref, act_ref, hn_ref, gate_hbm, up_hbm, down_hbm, w_gate, w_up, w_down, in_sems, out_sems = refs[2 * N_DEV :]
+    f32, bf16 = jnp.float32, jnp.bfloat16
+    me = lax.axis_index("fsdp")
+    rows_w, rows_d = wide_slots[0].shape[1], down_slots[0].shape[0]
+    outs = [pltpu.make_async_copy(src, dst, out_sems.at[i]) for i, (src, dst) in enumerate([(w_gate, gate_hbm), (w_up, up_hbm), (w_down, down_hbm)])]
+
+    @pl.when(pl.program_id(0) == 0)
+    def _():
+        copies = []
+        for step in range(N_DEV):
+            dev = peer_of(me, step)
+            copies.append(pltpu.make_async_copy(wide_slots[step].at[0], w_gate.at[pl.ds(dev * rows_w, rows_w)], in_sems.at[step, 0]))
+            copies.append(pltpu.make_async_copy(wide_slots[step].at[1], w_up.at[pl.ds(dev * rows_w, rows_w)], in_sems.at[step, 1]))
+            copies.append(pltpu.make_async_copy(down_slots[step], w_down.at[pl.ds(dev * rows_d, rows_d)], in_sems.at[step, 2]))
+        for copy in copies:
+            copy.start()
+        for copy in copies:
+            copy.wait()
+        for copy in outs:
+            copy.start()
+
+    emb = x_ref[...].astype(f32)
+    a_norm, _ = rms_scale(emb, gain1_ref[...])
+    for chunk in range(w_gate.shape[1] // 512):
+        cols = slice(chunk * 512, (chunk + 1) * 512)
+        gate = jnp.dot(a_norm, w_gate[:, cols], preferred_element_type=f32).astype(bf16)
+        up = jnp.dot(a_norm, w_up[:, cols], preferred_element_type=f32).astype(bf16)
+        gate_ref[:, cols] = gate
+        up_ref[:, cols] = up
+        wide = gate.astype(f32)
+        act_ref[:, cols] = (wide * jax.nn.sigmoid(wide) * up.astype(f32)).astype(bf16)
+    hid = (emb + jnp.dot(act_ref[...], w_down[...], preferred_element_type=f32)).astype(bf16)
+    hid_ref[...] = hid
+    hn_ref[...], _ = rms_scale(hid.astype(f32), gain2_ref[...])
+
+    @pl.when(pl.program_id(0) == pl.num_programs(0) - 1)
+    def _():
+        for copy in outs:
+            copy.wait()
+
+
+def forward_call(wide_slots, down_slots, x_rows, gain_mlp, gain_head, groups):
+    slots, width = groups * UNIT, x_rows.shape[1]
+    wide = wide_slots[0].shape[2]
+    bf16 = jnp.bfloat16
+    dma = pltpu.SemaphoreType.DMA
+    hbm = pl.BlockSpec(memory_space=pl.ANY)
+    gain = pl.BlockSpec((1, width), lambda i: (0, 0))
+    narrow = pl.BlockSpec((UNIT, width), lambda i: (i, 0))
+    broad = pl.BlockSpec((UNIT, wide), lambda i: (i, 0))
+    full = [(width, wide), (width, wide), (wide, width)]
+    return pl.pallas_call(
+        forward_kernel,
+        grid=(groups,),
+        out_shape=[jax.ShapeDtypeStruct(shape, bf16) for shape in [(slots, width), (slots, wide), (slots, wide), (slots, wide), (slots, width)] + full],
+        in_specs=[hbm] * (2 * N_DEV) + [narrow, gain, gain],
+        out_specs=[narrow, broad, broad, broad, narrow, hbm, hbm, hbm],
+        scratch_shapes=[pltpu.VMEM(shape, bf16) for shape in full] + [dma((N_DEV, 3)), dma((3,))],
+        compiler_params=pltpu.CompilerParams(vmem_limit_bytes=VMEM_MAX),
+        cost_estimate=pl.CostEstimate(flops=6 * slots * wide * width, bytes_accessed=6 * slots * wide, transcendentals=slots * wide),
+        name="block_forward",
+    )(*wide_slots, *down_slots, x_rows, gain_mlp.reshape(1, width), gain_head.reshape(1, width))
+
+
+def back_kernel(groups, dhn_ref, x_hbm, hid_hbm, gate_hbm, up_hbm, act_hbm, gain1_ref, gain2_ref, w_gate_hbm, w_up_hbm, w_down_hbm, rows_ref, head_hbm, lse_ref, pick_ref, norm_ref,
                 loss_out, dtable_ref, dgate_ref, dup_ref, ddown_ref,
-                x_buf, hid_buf, gate_buf, up_buf, act_buf, w_gate, w_up, w_down, head_buf, dh_wide, dh_narrow, dh_t, a_t, da_acc, dp_buf, dq_buf, dx_parts, inv_buf,
-                down_acc, down_core, down_first, down_second, wide_acc, wide_core, wide_first, wide_second, loss_all,
+                x_buf, hid_buf, gate_buf, up_buf, act_buf, w_gate, w_up, w_down, dh_wide, dh_narrow, dh_t, a_t, da_acc, dp_buf, dq_buf, dx_parts,
+                down_acc, down_core, down_first, down_second, wide_acc, wide_core, wide_first, wide_second, loss_all, loss_ref,
                 in_sems, tile_sems, loss_send, loss_recv, core_send, core_recv, first_send, first_recv, second_send, second_recv):
     me = lax.axis_index("fsdp")
     core = me % 2
     first_step = 2 + 2 * core
     second_step = 4 - 2 * core
-    chunk_w = 512
+    chunk_w = WIDE_CHUNK
     chunks = w_gate.shape[1] // chunk_w
     f32, bf16 = jnp.float32, jnp.bfloat16
 
-    whole = [(x_hbm, x_buf), (hid_hbm, hid_buf), (act_hbm, act_buf), (w_down_hbm, w_down), (w_gate_hbm, w_gate), (w_up_hbm, w_up), (head_hbm, head_buf)]
+    whole = [(x_hbm.at[pl.ds(0, groups * UNIT)], x_buf), (hid_hbm, hid_buf), (act_hbm, act_buf), (w_down_hbm, w_down), (w_gate_hbm, w_gate), (w_up_hbm, w_up), (head_hbm, dtable_ref)]
     loads = [pltpu.make_async_copy(src, dst, in_sems.at[i]) for i, (src, dst) in enumerate(whole)]
     tiles = [pltpu.make_async_copy(src, dst, tile_sems.at[i]) for i, (src, dst) in enumerate([(gate_hbm, gate_buf), (up_hbm, up_buf)])]
     for load in loads[:4] + tiles + loads[4:]:
         load.start()
+    nats = jnp.sum(jnp.sum(lse_ref[...], axis=0), axis=1, keepdims=True) * LN2
+    gold = jnp.sum(jnp.sum(pick_ref[...], axis=0, keepdims=True), axis=1, keepdims=True)
+    loss_ref[...] = jnp.broadcast_to(nats - gold, (8, 128)) * norm_ref[1:2, :]
     meet_all(me)
 
     def loss_copy(step):
         return remote(loss_ref, loss_all.at[step], loss_send.at[step], loss_recv.at[step], peer_of(me, step))
-
-    for step in range(1, N_DEV):
-        loss_copy(step).start()
 
     def piece(unit, step):
         if isinstance(unit, int) and unit == 0:
@@ -405,6 +511,8 @@
         a_t[:, rows] = a_norm.astype(f32).T.astype(bf16)
         da_acc[rows, :] = jnp.zeros((UNIT, 256), f32)
 
+    for step in range(1, N_DEV):
+        loss_copy(step).start()
     loads[2].wait()
 
     @pl.loop(0, N_DEV)
@@ -461,7 +569,7 @@
     add_first(chunks - 1)
     loads[6].wait()
     row_block = 512
-    blocks = head_buf.shape[0] // row_block
+    blocks = dtable_ref.shape[0] // row_block
     row_iota = lax.broadcasted_iota(jnp.int32, (row_block, UNIT), 0)
 
     def scatter_block(block):
@@ -469,7 +577,7 @@
         rows = pl.ds(pl.multiple_of(base, row_block), row_block)
         picks = jnp.concatenate([jnp.where(row_iota == rows_ref[group] - base, 1.0, 0.0).astype(bf16) for group in range(groups)], axis=1)
         parts = jnp.dot(picks, dx_parts[...], preferred_element_type=f32)
-        dtable_ref[rows, :] = head_buf[rows, :] + (parts[:, 0:256] + (parts[:, 256:512] + parts[:, 512:768]))
+        dtable_ref[rows, :] += (parts[:, 0:256] + (parts[:, 256:512] + parts[:, 512:768]))
 
     @pl.loop(0, blocks // 2)
     def _(block):
@@ -498,18 +606,18 @@
         second_copy(unit).wait_send()
 
 
-def back_call(d_hnorm, x_rows, hid, gate, up, act, gain_mlp, gain_head, w_gate, w_up, w_down, row_id, head_grad, loss_part):
+def back_call(d_hnorm, x_rows, hid, gate, up, act, gain_mlp, gain_head, w_gate, w_up, w_down, row_id, head_grad, lse, picked, norm_rows, variant):
     groups, _, width = d_hnorm.shape
     slots, wide = gate.shape
     vocab = head_grad.shape[0]
-    chunks = wide // 512
+    chunks = wide // WIDE_CHUNK
     units = chunks + 1
     f32, bf16 = jnp.float32, jnp.bfloat16
     dma = pltpu.SemaphoreType.DMA
     vmem = pl.BlockSpec(memory_space=pltpu.VMEM)
     hbm = pl.BlockSpec(memory_space=pl.ANY)
     piece_d = (wide // N_DEV, width)
-    piece_w = (2, width // N_DEV, 512)
+    piece_w = (2, width // N_DEV, WIDE_CHUNK)
     return pl.pallas_call(
         functools.partial(back_kernel, groups),
         out_shape=(
@@ -519,7 +627,7 @@
             jax.ShapeDtypeStruct((width // N_DEV, wide), f32),
             jax.ShapeDtypeStruct(piece_d, f32),
         ),
-        in_specs=[vmem, hbm, hbm, hbm, hbm, hbm, vmem, vmem, hbm, hbm, hbm, vmem, hbm, vmem],
+        in_specs=[vmem, hbm, hbm, hbm, hbm, hbm, vmem, vmem, hbm, hbm, hbm, vmem, hbm, vmem, vmem, vmem],
         out_specs=(vmem,) * 5,
         scratch_shapes=[
             pltpu.VMEM((slots, width), bf16),
@@ -530,16 +638,14 @@
             pltpu.VMEM((width, wide), bf16),
             pltpu.VMEM((width, wide), bf16),
             pltpu.VMEM((wide, width), bf16),
-            pltpu.VMEM((vocab, width), f32),
             pltpu.VMEM((slots, width), f32),
             pltpu.VMEM((slots, width), bf16),
             pltpu.VMEM((width, slots), bf16),
             pltpu.VMEM((width, slots), bf16),
             pltpu.VMEM((slots, width), f32),
-            pltpu.VMEM((slots, 512), bf16),
-            pltpu.VMEM((slots, 512), bf16),
+            pltpu.VMEM((slots, WIDE_CHUNK), bf16),
+            pltpu.VMEM((slots, WIDE_CHUNK), bf16),
             pltpu.VMEM((slots, 3 * width), bf16),
-            pltpu.VMEM((8, 128), f32),
             pltpu.VMEM((N_DEV,) + piece_d, f32),
             pltpu.VMEM((4,) + piece_d, f32),
             pltpu.VMEM((2,) + piece_d, f32),
@@ -549,6 +655,7 @@
             pltpu.VMEM((chunks, 2) + piece_w, f32),
             pltpu.VMEM((chunks,) + piece_w, f32),
             pltpu.VMEM((N_DEV, 8, 128), f32),
+            pltpu.VMEM((8, 128), f32),
             dma((7,)),
             dma((2,)),
             dma((N_DEV,)),
@@ -560,61 +667,67 @@
             dma((units,)),
             dma((units,)),
         ],
-        compiler_params=pltpu.CompilerParams(collective_id=2, has_side_effects=True, vmem_limit_bytes=VMEM_MAX),
+        compiler_params=pltpu.CompilerParams(collective_id=2 + 2 * variant, has_side_effects=True, vmem_limit_bytes=VMEM_MAX),
         cost_estimate=pl.CostEstimate(flops=16 * slots * wide * width, bytes_accessed=6 * slots * wide, transcendentals=slots * wide),
         name="back",
-    )(d_hnorm, x_rows, hid, gate, up, act, gain_mlp.reshape(1, width), gain_head.reshape(1, width), w_gate, w_up, w_down, row_id, head_grad, loss_part)
-
-
-GROUPS = 7
+    )(d_hnorm, x_rows, hid, gate, up, act, gain_mlp.reshape(1, width), gain_head.reshape(1, width), w_gate, w_up, w_down, row_id, head_grad, lse, picked, norm_rows)
+
+
+FEW_GROUPS, MANY_GROUPS = 6, 7
 
 
 def solution(mesh):
-    def gather_rows(row_shard):
-        return lax.all_gather(row_shard, "fsdp", axis=0, tiled=True)
+    def swap(values, step):
+        return lax.ppermute(values, "fsdp", [(dev, dev ^ step) for dev in range(N_DEV)])
+
 
     def device_step(tok_ids, tok_labels, loss_mask, table_shard, gain_mlp, gain_head, gate_shard, up_shard, down_shard):
-        me = lax.axis_index("fsdp")
         vocab, width = table_shard.shape
         vocab_all = vocab * N_DEV
-        slots = GROUPS * UNIT
-        gate_full, up_full, down_full = gather_rows(gate_shard), gather_rows(up_shard), gather_rows(down_shard)
-        block = jnp.stack([tok_ids.reshape(-1, 128), tok_labels.reshape(-1, 128), loss_mask.reshape(-1, 128)])
-        every = gather_tokens(block)
-        ids, labels, mask = every[:, 0].reshape(-1), every[:, 1].reshape(-1), every[:, 2].reshape(-1)
-        count = jnp.sum(mask).astype(jnp.float32)
-        owner = ids // vocab
-        loads = [jnp.sum(jnp.where(owner == dev, mask, 0)) for dev in range(N_DEV)]
-        rounds = (functools.reduce(jnp.maximum, loads) + slots - 1) // slots
-        last = jnp.int32(2**31 - 1)
-        packed = jnp.where((owner == me) & (mask != 0), (ids - me * vocab) * vocab_all + labels, last)
-        packed = jnp.sort(packed)
-        most = -(-ids.shape[0] // slots) * slots
-        packed = jnp.concatenate([packed, jnp.full((most - ids.shape[0],), last)])
-        norm_rows = jnp.zeros((8, 128), jnp.float32).at[0].set(jnp.log2(count)).at[1].set(1.0 / count)
-        table_t = table_shard.T
-
-        def one_round(turn):
-            mine = lax.dynamic_slice(packed, (turn * slots,), (slots,))
-            valid = mine != last
+
+        def row_part(mine):
+            valid = mine != LAST_KEY
             row_id = jnp.where(valid, mine // vocab_all, 0)
-            label = jnp.where(valid, mine % vocab_all, -1)
-            x_rows = jnp.take(table_shard, row_id, axis=0)
-            (hid, gate, up, act), h_norm = mlp_forward(x_rows, gain_mlp, gain_head, gate_full, up_full, down_full)
-            d_hnorm, head_grad, lse, picked = head_call(h_norm.reshape(GROUPS, UNIT, width), label.reshape(GROUPS, 1, UNIT), norm_rows, table_shard, table_t, GROUPS)
-            part = (jnp.sum(lse) * LN2 - jnp.sum(picked)) / count
-            loss_part = jnp.broadcast_to(part, (8, 128))
-            return back_call(d_hnorm, x_rows, hid, gate, up, act, gain_mlp, gain_head, gate_full, up_full, down_full, row_id.reshape(GROUPS, 1, UNIT), head_grad, loss_part)
-
-        def more_rounds(sums):
+            return row_id, jnp.where(valid, mine % vocab_all, -1), jnp.take(table_shard, row_id, axis=0)
+
+        packed, info, table_t = gather_tokens(tok_ids, tok_labels, loss_mask, table_shard)
+        own, packed = lax.optimization_barrier(((jnp.stack([gate_shard, up_shard]), down_shard), packed))
+        even = [own] + [tuple(swap(block, step) for block in own) for step in (2, 4, 6)]
+        many_slots = MANY_GROUPS * UNIT
+        packed = jnp.sort(packed.reshape(-1))
+        first = row_part(packed[:many_slots])
+        even, first = lax.optimization_barrier((even, first))
+        odd = [tuple(swap(block, 1) for block in slot) for slot in even]
+        wide_slots, down_slots = zip(*[slot for two in zip(even, odd) for slot in two])
+        most_load = info[2, 0].astype(jnp.int32)
+
+        def one_round(groups, variant, rows):
+            slots = groups * UNIT
+            row_id, label, x_rows = rows[0][:slots], rows[1][:slots], rows[2]
+            hid, gate, up, act, h_norm, gate_full, up_full, down_full = forward_call(wide_slots, down_slots, x_rows, gain_mlp, gain_head, groups)
+            d_hnorm, head_grad, lse, picked = head_call(h_norm.reshape(groups, UNIT, width), label.reshape(groups, 1, UNIT), info, table_shard, table_t, groups, variant)
+            return tuple(back_call(d_hnorm, x_rows, hid, gate, up, act, gain_mlp, gain_head, gate_full, up_full, down_full, row_id.reshape(groups, 1, UNIT), head_grad, lse, picked, info, variant))
+
+        rounds = (most_load + many_slots - 1) // many_slots
+        keys = jnp.concatenate([packed, jnp.full((-packed.shape[0] % many_slots,), LAST_KEY, jnp.int32)])
+
+        def few():
+            return one_round(FEW_GROUPS, 0, first)
+
+        def many():
+            return one_round(MANY_GROUPS, 1, first)
+
+        def several():
             def step(state):
-                extra = one_round(state[0])
+                extra = one_round(MANY_GROUPS, 1, row_part(lax.dynamic_slice(keys, (state[0] * many_slots,), (many_slots,))))
                 return (state[0] + 1, tuple(old + new for old, new in zip(state[1], extra)))
 
-            return lax.while_loop(lambda state: state[0] < rounds, step, (jnp.int32(1), tuple(sums)))[1]
-
-        sums = lax.cond(rounds > 1, more_rounds, tuple, one_round(jnp.int32(0)))
-        loss, g_table, g_gate, g_up, g_down = sums
+            shapes = jax.eval_shape(many)
+            zeros = tuple(jnp.zeros(shape.shape, shape.dtype) for shape in shapes)
+            return lax.while_loop(lambda state: state[0] < rounds, step, (jnp.int32(0), zeros))[1]
+
+        branch = (most_load > FEW_GROUPS * UNIT).astype(jnp.int32) + (rounds > 1).astype(jnp.int32)
+        loss, g_table, g_gate, g_up, g_down = lax.switch(branch, [few, many, several])
         return (loss[0, 0], g_table, g_gate, g_up, g_down)
 
     row_spec = P("fsdp", None)

time: 409 us -> 321 us (0.78)
  Pallas kernels: 313 us -> 264 us
  matrix products: 22.4 us -> 0 us
  between operations: 21.3 us -> 1.63 us
  starting transfers between devices: 0.11 us -> 8.82 us
  loops' own time: 1.72 us -> 7.6 us
  other arithmetic: 16.5 us -> 11.6 us
    pallas_call x1, Pallas kernels: 245 us -> 187 us  [head_call(): pl.pallas_call(functools.partial(head_kernel, groups, vocab), out_shape=(...]
    dot_general x3 -> x0, matrix products: 22.4 us -> none  [the longest x1 10.5 us: mlp_forward(): jnp.dot(a_norm, w_up, preferred_element_type=jnp.float32)]
    pallas_call x1 -> x2, Pallas kernels: 8.46 us -> 23.2 us  [the longest x1 13.8 us: forward_call(): pl.pallas_call(forward_kernel, grid=(groups,), out_shape=[jax.ShapeDtypeS...]
    ppermute x0 -> x14, starting transfers between devices: none -> 8.82 us  [swap(): lax.ppermute(values, 'fsdp', [(dev, dev ^ step) for dev in range(N_DEV)])]
    another operation x1, loops' own time: 1.72 us -> 7.6 us  [device_step(): lax.switch(branch, [few, many, several])]
    reduce_sum x4 -> x0, other arithmetic: 5.2 us -> none  [the longest x2 2.64 us: one_round(): part = (jnp.sum(lse) * LN2 - jnp.sum(picked)) / count]
    all_gather x3 -> x0, waiting for transfers between devices: 5.06 us -> none  [gather_rows(): return lax.all_gather(row_shard, 'fsdp', axis=0, tiled=True)]
    unnamed x25 -> x10, local copies, waits for them, and re-layouts: 11.7 us -> 6.66 us
  transfers between devices with their start and end apart: 3 -> 14, of which waited for: 1 -> 2; matrix products, arithmetic and copies ran while one was open for 10% -> 5% of each run, Pallas kernels for 2% -> 0%
where the time goes in v3:
time: 321 us; the launch traced here: 315 us
  Pallas kernels  264 us (82%)
  local copies, waits for them, and re-layouts  16.6 us (5%)
  other arithmetic  11.6 us (4%)
  starting transfers between devices  8.82 us (3%)
  loops' own time  7.6 us (2%)
  waiting for transfers between devices  4.68 us (1%)
    pallas_call x1, Pallas kernels, head_call(): pl.pallas_call(functools.partial(head_kernel, groups, vocab), out_shape=(...  187 us
    pallas_call x1, Pallas kernels, back_call(): pl.pallas_call(functools.partial(back_kernel, groups), out_shape=(jax.Sha...  54.3 us
    pallas_call x1, Pallas kernels, forward_call(): pl.pallas_call(forward_kernel, grid=(groups,), out_shape=[jax.ShapeDtypeS...  13.8 us
    pallas_call x1, Pallas kernels, gather_tokens(): pl.pallas_call(tokens_kernel, out_shape=(jax.ShapeDtypeStruct((N_DEV,) +...  9.41 us
    ppermute x14, starting transfers between devices, swap(): lax.ppermute(values, 'fsdp', [(dev, dev ^ step) for dev in range(N_DEV)])  8.82 us
    sort x1, other arithmetic, device_step(): packed = jnp.sort(packed.reshape(-1))  8.6 us
    another operation x1, loops' own time, device_step(): lax.switch(branch, [few, many, several])  7.6 us
    unnamed x10, local copies, waits for them, and re-layouts  6.66 us
  transfers between devices with their start and end apart: 14, of which 2 were waited for; matrix products, arithmetic and copies ran while one was open for 5% of the time, Pallas kernels for 0%

profile of v3, /device:TPU:0, one launch (start us, length us, event | category | flops | bytes accessed | tf_op | source)
XLA Modules:
  0.0 315.1 jit_solution(14210354577693601293)
XLA Ops:
  0.6 1.7 pad_maximum_fusion
  2.3 9.4 %gather_tokens.1 = (s32[8,16,128]{2,1,0:T(8,128)}, f32[8,128]{1,0:T(8,128)}, bf16[256,4096]{1,0:T(8,128)(2,1)}) custom-call(s32[16,128]{1,0:T(8,128)} %bitcast.32, s32[16,128]{1,0:T(8,128)} %bitcast.33, s32[16,128]{1,0:T(8,128)} %bitcast.34, bf16[4096,256]{1,0:T(8,128)(2,1)} %table_hbm.1), custom_call_target="tpu_custom_call" | custom-call | tf_op jit(solution)/shard_map/gather_tokens/pallas_call | solution.py:97
  11.7 2.4 collective-permute-start.5
  14.2 0.6 collective-permute-start.3
  14.7 1.5 collective-permute-start.4
  16.2 0.5 collective-permute-start.2
  16.7 1.5 collective-permute-start
  18.2 8.6 %sort.15 = (s32[16384]{0:T(1024)S(1)}, s32[16384]{0:T(1024)}) sort(s32[16384]{0:T(1024)} %bitcast.31, s32[16384]{0:T(1024)S(1)} %iota.3), dimensions={0}, to_apply=%region_0.0 | sort | flops 229376 | bytes 262144 | tf_op jit(solution)/shard_map/jit(sort)/sort | solution.py:697
  26.9 6.0 %gather_fusion.1 = bf16[1792,256]{1,0:T(8,128)(2,1)S(1)} fusion(bf16[4096,256]{1,0:T(8,128)(2,1)} %table_hbm.1, s32[2048]{0:T(1024)S(1)} %pad_clamp_fusion.1), kind=kCustom, calls=%fused_computation.1 | custom fusion | bytes 1842176 | tf_op jit(solution)/shard_map/jit(_take)/gather | solution.py:691
  32.9 1.3 broadcast_select_fusion.1
  34.2 0.0 collective-permute-done.5
  34.2 0.5 collective-permute-start.1
  34.8 0.0 collective-permute-done.3
  34.8 4.4 %collective-permute-done.1 = bf16[256,256]{1,0:T(8,128)(2,1)S(1)} collective-permute-done((bf16[256,256]{1,0:T(8,128)(2,1)}, bf16[256,256]{1,0:T(8,128)(2,1)S(1)}, u32[]{:S(2)}, u32[]{:S(2)}) %collective-permute-start.1) | collective-permute-done | bytes 131104 | tf_op jit(solution)/shard_map/ppermute | solution.py:681
  39.2 0.0 collective-permute-done.4
  39.2 0.0 collective-permute-done.2
  39.2 0.0 collective-permute-done
  39.2 0.0 collective-permute-start.10
  39.2 0.5 collective-permute-start.11
  39.7 0.0 collective-permute-start.12
  39.8 0.5 collective-permute-start.6
  40.2 0.0 collective-permute-start.7
  40.3 0.2 collective-permute-done.10
  40.5 0.2 collective-permute-start.8
  40.7 0.0 collective-permute-done.11
  40.7 0.3 collective-permute-start.9
  41.0 0.0 collective-permute-done.12
  41.0 0.2 collective-permute-start.13
  41.3 1.2 slice.39
  43.1 0.0 collective-permute-done.13
  43.1 0.0 collective-permute-done.6
  43.2 0.0 collective-permute-done.7
  43.2 0.0 collective-permute-done.8
  43.2 0.0 collective-permute-done.9
  43.2 263.9 %conditional.1 = (f32[4096,256]{1,0:T(8,128)}, f32[32,2048]{1,0:T(8,128)}, f32[32,2048]{1,0:T(8,128)}, f32[256,256]{1,0:T(8,128)}, f32[8,128]{1,0:T(8,128)}) conditional(s32[]{:T(128)} %clamp.3, (f32[256]{0:T(256)}, f32[256]{0:T(256)}, bf16[2,32,2048]{2,1,0:T(8,128)(2,1)}, bf16[2,32,2048]{2,1,0:T(8,128)(2,1)}, ...), branch_computations={%region_1.2_spmd, %region_2.3_spmd, %region_3.6_spmd} | conditional | flops 140930383872 | bytes 94156328 | solution.py:730
  43.5 0.0 copy-start.5
  43.5 0.0 copy-start.9
  43.5 0.0 copy-start.13
  43.5 0.0 copy-start.17
  43.5 0.0 copy-start.21
  43.5 0.0 copy-start.25
  43.6 0.7 slice.33.lab_hbm
  44.3 0.0 copy-done.5
  44.3 0.0 copy-done.9
  44.3 0.1 copy-done.13
  44.4 0.0 copy-done.17
  44.4 0.0 copy-done.21
  44.4 0.0 copy-done.25
  44.5 0.6 slice.35.rows_ref
  45.1 13.8 %block_forward.6 = (bf16[1536,256]{1,0:T(8,128)(2,1)}, bf16[1536,2048]{1,0:T(8,128)(2,1)}, bf16[1536,2048]{1,0:T(8,128)(2,1)}, bf16[1536,2048]{1,0:T(8,128)(2,1)...) custom-call(bf16[2,32,2048]{2,1,0:T(8,128)(2,1)} %get-tuple-element., ...), custom_call_target="tpu_custom_call" | custom-call | flops 4831838208 | bytes 18874368 | tf_op jit(solution)/shard_map/cond/branch_0_fun/block_forward/pallas_call | solution.py:410
  58.9 186.6 %head.6 = (f32[6,256,256]{2,1,0:T(8,128)}, f32[4096,256]{1,0:T(8,128)}, f32[6,1,256]{2,1,0:T(1,128)}, f32[8,512]{1,0:T(8,128)}) custom-call(bf16[6,256,256]{2,1,0:T(8,128)(2,1)} %bitcast.49, s32[6,1,256]{2,1,0:T(1,128)} %slice.33.lab_hbm, f32[8,128]{1,0:T(8,128)} %get-tuple-element.490.norm_ref, bf16[4096,256]{1,0:T(8,128)(2,1)} %get-tuple-element.491.table_ref, ...), custom_call_target="tpu_custom_call" | custom-call | flops 103079215104 | bytes 16777216 | tf_op jit(solution)/shard_map/cond/branch_0_fun/head/pallas_call | solution.py:313
  245.5 54.3 %back.6 = (f32[8,128]{1,0:T(8,128)}, f32[4096,256]{1,0:T(8,128)}, f32[32,2048]{1,0:T(8,128)}, f32[32,2048]{1,0:T(8,128)}, f32[256,256]{1,0:T(8,128)}) custom-call(f32[6,256,256]{2,1,0:T(8,128)} %get-tuple-element.493.dhn_ref, bf16[1792,256]{1,0:T(8,128)(2,1)} %get-tuple-element.485.refs_16_.x_hbm, bf16[1536,256]{1,0:T(8,128)(2,1)} %get-tuple-element.494.hid_hbm, ...), custom_call_target="tpu_custom_call" | custom-call | flops 12884901888 | bytes 18874368 | tf_op jit(solution)/shard_map/cond/branch_0_fun/back/pallas_call | solution.py:621
  307.1 1.2 slice.41
  308.3 0.0 copy-start
  308.3 0.0 copy-start.1
  308.3 0.0 copy-start.2
  308.3 4.5 %copy.51 = f32[4096,256]{1,0:T(8,128)} copy(f32[4096,256]{1,0:T(8,128)} %get-tuple-element.1085) | data formatting | bytes 8388608
  312.8 0.0 copy-done
  312.8 0.7 copy.52
  313.5 0.0 copy-done.1
  313.5 0.7 copy.53
  314.2 0.0 copy-done.2
  314.2 0.7 copy.54
  (5 shorter events, 0.0 us)
Async XLA Ops:
  11.7 22.5 %collective-permute-start.5 = (bf16[256,256]{1,0:T(8,128)(2,1)}, bf16[256,256]{1,0:T(8,128)(2,1)S(1)}, u32[]{:S(2)}, u32[]{:S(2)}) collective-permute-start(bf16[256,256]{1,0:T(8,128)(2,1)} %param.22), channel_id=1, source_target_pairs={{0,6},{1,7},{2,4},{3,5},{4,2},{5,3},{6,0},{7,1}} | collective-permute-start | bytes 393224 | tf_op jit(solution)/shard_map/ppermute | solution.py:681
  14.2 20.6 %collective-permute-start.3 = (bf16[256,256]{1,0:T(8,128)(2,1)}, bf16[256,256]{1,0:T(8,128)(2,1)S(1)}, u32[]{:S(2)}, u32[]{:S(2)}) collective-permute-start(bf16[256,256]{1,0:T(8,128)(2,1)} %param.22), channel_id=1, source_target_pairs={{0,4},{1,5},{2,6},{3,7},{4,0},{5,1},{6,2},{7,3}} | collective-permute-start | bytes 393224 | tf_op jit(solution)/shard_map/ppermute | solution.py:681
  14.7 24.5 %collective-permute-start.4 = (bf16[2,32,2048]{2,1,0:T(8,128)(2,1)}, bf16[2,32,2048]{2,1,0:T(8,128)(2,1)S(1)}, u32[]{:S(2)}, u32[]{:S(2)}) collective-permute-start(bf16[2,32,2048]{2,1,0:T(8,128)(2,1)} %pad_maximum_fusion), channel_id=1, source_target_pairs={{0,6},{1,7},{2,4},{3,5},{4,2},{5,3},{6,0},{7,1}} | collective-permute-start | bytes 786440 | tf_op jit(solution)/shard_map/ppermute | solution.py:681
  16.2 23.0 %collective-permute-start.2 = (bf16[2,32,2048]{2,1,0:T(8,128)(2,1)}, bf16[2,32,2048]{2,1,0:T(8,128)(2,1)S(1)}, u32[]{:S(2)}, u32[]{:S(2)}) collective-permute-start(bf16[2,32,2048]{2,1,0:T(8,128)(2,1)} %pad_maximum_fusion), channel_id=1, source_target_pairs={{0,4},{1,5},{2,6},{3,7},{4,0},{5,1},{6,2},{7,3}} | collective-permute-start | bytes 786440 | tf_op jit(solution)/shard_map/ppermute | solution.py:681
  16.7 22.5 %collective-permute-start = (bf16[2,32,2048]{2,1,0:T(8,128)(2,1)}, bf16[2,32,2048]{2,1,0:T(8,128)(2,1)S(1)}, u32[]{:S(2)}, u32[]{:S(2)}) collective-permute-start(bf16[2,32,2048]{2,1,0:T(8,128)(2,1)} %pad_maximum_fusion), channel_id=1, source_target_pairs={{0,2},{1,3},{2,0},{3,1},{4,6},{5,7},{6,4},{7,5}} | collective-permute-start | bytes 786440 | tf_op jit(solution)/shard_map/ppermute | solution.py:681
  34.2 5.0 %collective-permute-start.1 = (bf16[256,256]{1,0:T(8,128)(2,1)}, bf16[256,256]{1,0:T(8,128)(2,1)S(1)}, u32[]{:S(2)}, u32[]{:S(2)}) collective-permute-start(bf16[256,256]{1,0:T(8,128)(2,1)} %param.22), channel_id=1, source_target_pairs={{0,2},{1,3},{2,0},{3,1},{4,6},{5,7},{6,4},{7,5}} | collective-permute-start | bytes 393224 | tf_op jit(solution)/shard_map/ppermute | solution.py:681
  39.2 1.3 collective-permute-start.10
  39.2 1.5 collective-permute-start.11
  39.7 1.3 collective-permute-start.12
  39.8 3.4 %collective-permute-start.6 = (bf16[2,32,2048]{2,1,0:T(8,128)(2,1)}, bf16[2,32,2048]{2,1,0:T(8,128)(2,1)}, u32[]{:S(2)}, u32[]{:S(2)}) collective-permute-start(bf16[2,32,2048]{2,1,0:T(8,128)(2,1)} %pad_maximum_fusion), channel_id=1, source_target_pairs={{0,1},{1,0},{2,3},{3,2},{4,5},{5,4},{6,7},{7,6}} | collective-permute-start | bytes 786440 | tf_op jit(solution)/shard_map/ppermute | solution.py:681
  40.2 2.9 collective-permute-start.7
  40.5 2.7 collective-permute-start.8
  40.7 2.4 collective-permute-start.9
  41.0 2.1 collective-permute-start.13
  43.5 0.8 copy-start.5
  43.5 0.8 copy-start.9
  43.5 0.9 copy-start.13
  43.5 0.9 copy-start.17
  43.5 0.9 copy-start.21
  43.5 0.9 copy-start.25
  308.3 4.6 %copy-start = (f32[32,2048]{1,0:T(8,128)S(1)}, f32[32,2048]{1,0:T(8,128)}, u32[]{:S(2)}) copy-start(f32[32,2048]{1,0:T(8,128)} %get-tuple-element.1086) | copy-start | bytes 786436
  308.3 5.3 %copy-start.1 = (f32[32,2048]{1,0:T(8,128)S(1)}, f32[32,2048]{1,0:T(8,128)}, u32[]{:S(2)}) copy-start(f32[32,2048]{1,0:T(8,128)} %get-tuple-element.1087) | copy-start | bytes 786436
  308.3 6.0 %copy-start.2 = (f32[256,256]{1,0:T(8,128)S(1)}, f32[256,256]{1,0:T(8,128)}, u32[]{:S(2)}) copy-start(f32[256,256]{1,0:T(8,128)} %get-tuple-element.1088) | copy-start | bytes 786436
